TPU v7x, 256 devices: a whole 4x4x8 slice. The times are simulated.
256 devices in a mesh: gx: 8 (over x_hi, y), gy: 4 (over x_lo, core), gz: 8 (over z).
Axes of the slice: x: 4 (x_hi: 2, x_lo: 2; x = x_hi * 2 + x_lo), y: 4, z: 8, core: 2. Of those that a mesh axis runs over, the one named last changes fastest.
Arguments:
- node_latents: bfloat16 [262144, 128], P(('gx', 'gy', 'gz')), may hold values from -300 to 300
- cluster_latents: bfloat16 [65536, 128], P(('gx', 'gy', 'gz')), may hold values from -6 to 6
- senders: int32 [8192, 128], P(('gx', 'gy', 'gz')), may hold values from 0 to 4095
- membership: int32 [262144], P(('gx', 'gy', 'gz')), may hold values from 0 to 255
- w_key: bfloat16 [128, 128], replicated, may hold values from -1 to 1
- w_value: bfloat16 [128, 128], replicated, may hold values from -0.5 to 0.5
- w_edge_in: bfloat16 [256, 128], replicated, may hold values from -0.375 to 0.375
- w_edge_out: bfloat16 [128, 128], replicated, may hold values from -0.5 to 0.5
- w_node_in: bfloat16 [512, 128], replicated, may hold values from -0.25 to 0.25
- w_node_out: bfloat16 [128, 128], replicated, may hold values from -0.5 to 0.5
- out_gain: float32 [128], replicated, may hold values from 0.5 to 1.5
Outputs:
- new_latents: bfloat16 [262144, 128], P(('gx', 'gy', 'gz'))
All inputs are finite; a program needn't handle non-finite values.
Results may differ from a plain program's by a relative error of at most 0.005.
Values may be sent and summed in bfloat16 or wider, within the bound.
No kernel may reach another device: no remote copies, remote signals or barrier semaphores. Data moves between devices by JAX's collectives and lax.ppermute only.
A program may use at most 64 MiB of HBM per device.

v0:
```python
import math

import jax
import jax.numpy as jnp
from jax import lax
from jax.experimental import pallas as pl
from jax.experimental.pallas import tpu as pltpu
from jax.sharding import PartitionSpec as P


BND = 512
F32 = jnp.float32
BF16 = jnp.bfloat16
TILE = 128
ROWS = 256
VMEM_BYTES = 20 * 2**20

VMEM = pl.BlockSpec(memory_space=pltpu.VMEM)
SMEM = pl.BlockSpec(memory_space=pltpu.SMEM)

W_KEY, W_VALUE, _, W_SEND, W_MSG, _, W_AGG, W_ATT, _, W_OUT = range(10)


def near(x):
    return pltpu.with_memory_space_constraint(x, pltpu.VMEM)


def dot(a, b):
    return jnp.dot(a, b, preferred_element_type=F32)


def silu(x):
    return x * 0.5 * (1.0 + jnp.tanh(x * 0.5))


def weight(stacked, which):
    width = stacked.shape[1]
    return stacked[which * width : (which + 1) * width, :]


def scale_of(width):
    return math.log2(math.e) / math.sqrt(width)


def row_loop(count, body):
    def step(r, _):
        body(pl.ds(pl.multiple_of(r * ROWS, ROWS), ROWS))
        return 0

    lax.fori_loop(0, count // ROWS, step, 0)


def project(pieces, weights, keys, values):
    width = weights.shape[1]
    at = 0
    for piece in pieces:
        n = piece.shape[0]
        keys[:, at : at + n] = dot(piece[...], weight(weights, W_KEY)).astype(BF16).T
        values[at : at + n, 0:width] = dot(piece[...], weight(weights, W_VALUE)).astype(BF16)
        values[at : at + n, width : 2 * width] = jnp.ones((n, width), BF16)
        at += n


def wide(x, copies):
    return jnp.concatenate([x] * copies, axis=1)


def absorb(q, keys, values, top, acc):
    width = q.shape[1]
    scale = scale_of(width)
    scores = dot(q, keys)
    highest = jnp.broadcast_to(jnp.max(scores, axis=1, keepdims=True), (q.shape[0], width))
    newest = highest if top is None else jnp.maximum(top, highest)
    weights = jnp.exp2((scores - wide(newest, scores.shape[1] // width)) * scale).astype(BF16)
    part = dot(weights, values)
    if top is not None:
        part = acc * wide(jnp.exp2((top - newest) * scale), 2) + part
    return newest, part


def load_kernel(
    own_far, clusters_far, member_far, gain_far, own, clusters, border, both, member, gain, done
):
    head = own_far.at[:BND, :]
    copies = [
        pltpu.make_async_copy(source, target, done.at[at])
        for at, (source, target) in enumerate(
            (
                (head, both.at[:BND, :]),
                (clusters_far, both.at[BND:, :]),
                (head, border),
                (clusters_far, clusters),
                (member_far, member),
                (gain_far, gain),
                (own_far, own),
            )
        )
    ]
    for copy in copies:
        copy.start()
    for copy in copies:
        copy.wait()


def stack_kernel(*refs):
    *pieces, out = refs
    at = 0
    for piece in pieces:
        out[at : at + piece.shape[0], :] = piece[...]
        at += piece.shape[0]


def stack_after_border_kernel(border, clusters, came, out):
    n = clusters.shape[0]
    out[:BND, :] = border[...]
    out[BND : BND + n, :] = clusters[...]
    out[BND + n :, :] = came[BND:, :]


def prep_kernel(
    own, clusters, member, w_key, w_value, w_in, w_msg, w_node, w_out,
    weights, recv, base, top, acc, keys, values,
):
    count, width = own.shape
    at = 0
    for w in (w_key, w_value, w_in, w_msg, w_node, w_out):
        weights[at : at + w.shape[0], :] = w[...]
        at += w.shape[0]
    project((clusters,), weights, keys, values)
    columns = member[...].T
    lanes = lax.broadcasted_iota(jnp.int32, (TILE, clusters.shape[0]), 1)
    for t in range(count // TILE):
        here = pl.ds(t * TILE, TILE)
        q = own[here, :]
        one_hot = (columns[:, t : t + 1] == lanes).astype(BF16)
        own_cluster = dot(one_hot, clusters[...]).astype(BF16)
        base[here, :] = dot(q, weight(w_node, 0)) + dot(own_cluster, weight(w_node, 3))
        recv[here, :] = dot(q, w_in[:width, :])
        top[here, :], acc[here, :] = absorb(q, keys[...], values[...], None, None)


def edge_kernel(senders, own, xa, xb, ya, yb, za, zb, weights, recv, base, out, table, rows):
    count, _ = own.shape
    w_send = weight(weights, W_SEND)
    table[0:count, :] = dot(own[...], w_send)
    for at, axis, pair in ((0, "gx", (xa, xb)), (2, "gy", (ya, yb)), (4, "gz", (za, zb))):
        odd = lax.axis_index(axis) % 2
        low = pl.multiple_of(count + BND * (at + 1 - odd), BND)
        high = pl.multiple_of(count + BND * (at + odd), BND)
        table[pl.ds(low, BND), :] = dot(pair[0][:BND, :], w_send)
        table[pl.ds(high, BND), :] = dot(pair[1][:BND, :], w_send)
    w_sum = jnp.concatenate([weight(weights, W_MSG)] * 4, axis=0)

    def tile(t, _):
        def gather(g, _):
            for j in range(16):
                for d in range(4):
                    index = senders[t * TILE * 4 + g * 64 + j * 4 + d]
                    rows[d, pl.ds(pl.multiple_of(g * 16, 16) + j, 1), :] = table[pl.ds(index, 1), :]
            return 0

        lax.fori_loop(0, TILE // 16, gather, 0)
        here = pl.ds(pl.multiple_of(t * TILE, TILE), TILE)
        r = recv[here, :]
        hidden = jnp.concatenate([silu(rows[d] + r).astype(BF16) for d in range(4)], axis=1)
        agg = dot(hidden, w_sum).astype(BF16)
        out[here, :] = base[here, :] + dot(agg, weight(weights, W_AGG))
        return 0

    lax.fori_loop(0, count // TILE, tile, 0)


def middle_kernel(own, weights, top0, acc0, y0, y1, x0, x1, z0, z1, line_y, top_x, acc_x, top_z, acc_z, keys, values):
    count, width = own.shape
    n = x0.shape[0]
    project((y0.at[BND:, :], y1.at[BND:, :], x0, x1, z0, z1), weights, keys, values)

    def rows(here):
        q = own[here, :]
        t0, a0 = top0[here, :], acc0[here, :]
        _, a = absorb(q, keys[:, 0 : 3 * n], values[0 : 3 * n, :], t0, a0)
        line_y[here, :] = a[:, :width] / a[:, width:]
        top_x[here, :], acc_x[here, :] = absorb(q, keys[:, 3 * n : 6 * n], values[3 * n : 6 * n, :], t0, a0)
        top_z[here, :], acc_z[here, :] = absorb(q, keys[:, 6 * n : 9 * n], values[6 * n : 9 * n, :], t0, a0)

    row_loop(count, rows)


def final_kernel(own, weights, gain, base, line_y, top_x, acc_x, top_z, acc_z, x2, z2, out, keys, values):
    count, width = own.shape
    n = x2.shape[0]
    project((x2, z2), weights, keys, values)

    def rows(here):
        q = own[here, :]
        _, ax = absorb(q, keys[:, 0:n], values[0:n, :], top_x[here, :], acc_x[here, :])
        _, az = absorb(q, keys[:, n : 2 * n], values[n : 2 * n, :], top_z[here, :], acc_z[here, :])
        pooled = line_y[here, :] + ax[:, :width] / ax[:, width:] + az[:, :width] / az[:, width:]
        attended = (
            pooled * lax.rsqrt(jnp.mean(pooled * pooled, axis=1, keepdims=True) + 1e-06)
        ).astype(BF16)
        preact = base[here, :] + dot(attended, weight(weights, W_ATT))
        update = dot(silu(preact).astype(BF16), weight(weights, W_OUT))
        centred = update - jnp.mean(update, axis=1, keepdims=True)
        variance = jnp.mean(centred * centred, axis=1, keepdims=True)
        normed = centred * lax.rsqrt(variance + 1e-05)
        out[here, :] = (q.astype(F32) + normed * gain[...]).astype(BF16)

    row_loop(count, rows)


def call(kernel, args, outs, scratch=(), scalars=(), local=True):
    space = pltpu.VMEM if local else jax.ShapeDtypeStruct
    many = isinstance(outs, list)
    return pl.pallas_call(
        kernel,
        out_shape=[space(*o) for o in outs] if many else space(*outs),
        in_specs=[SMEM] * len(scalars) + [VMEM] * len(args),
        out_specs=[VMEM] * len(outs) if many else VMEM,
        scratch_shapes=[pltpu.VMEM(*s) for s in scratch],
        compiler_params=pltpu.CompilerParams(vmem_limit_bytes=VMEM_BYTES),
    )(*scalars, *map(near, args))


def exchange(x, axis, partner):
    size = lax.axis_size(axis)
    return lax.ppermute(x, axis, [(i, partner(i) % size) for i in range(size)])


def other_side(i):
    return i + 1 if i % 2 else i - 1


def on_device(
    node_latents,
    cluster_latents,
    senders,
    membership,
    w_key,
    w_value,
    w_edge_in,
    w_edge_out,
    w_node_in,
    w_node_out,
    out_gain,
):
    count, width = node_latents.shape
    n = cluster_latents.shape[0]

    def stack(pieces):
        return call(stack_kernel, pieces, ((sum(p.shape[0] for p in pieces), width), BF16))

    z0 = exchange(cluster_latents, "gz", lambda i: i ^ 4)
    x0 = exchange(cluster_latents, "gx", lambda i: i ^ 2)
    own, clusters, border, both, member, gain = pl.pallas_call(
        load_kernel,
        out_shape=[
            pltpu.VMEM((count, width), BF16),
            pltpu.VMEM((n, width), BF16),
            pltpu.VMEM((BND, width), BF16),
            pltpu.VMEM((BND + n, width), BF16),
            pltpu.VMEM((count // TILE, TILE), jnp.int32),
            pltpu.VMEM((1, width), F32),
        ],
        in_specs=[pl.BlockSpec(memory_space=pltpu.HBM)] * 4,
        out_specs=[VMEM] * 6,
        scratch_shapes=[pltpu.SemaphoreType.DMA((7,))],
        compiler_params=pltpu.CompilerParams(vmem_limit_bytes=VMEM_BYTES),
        name="load",
    )(
        *(
            pltpu.with_memory_space_constraint(x, pltpu.HBM)
            for x in (
                node_latents,
                cluster_latents,
                membership.reshape(count // TILE, TILE),
                out_gain.reshape(1, width),
            )
        )
    )
    y0 = exchange(both, "gy", lambda i: i ^ 1)
    za = exchange(border, "gz", lambda i: i ^ 1)
    xa = exchange(border, "gx", lambda i: i ^ 1)
    zb = exchange(border, "gz", other_side)
    xb = exchange(border, "gx", other_side)

    weights, recv, base, top, acc = call(
        prep_kernel,
        (
            own,
            clusters,
            member,
            w_key,
            w_value,
            w_edge_in,
            w_edge_out,
            w_node_in,
            w_node_out,
        ),
        [
            ((10 * width, width), BF16),
            ((count, width), F32),
            ((count, width), F32),
            ((count, width), F32),
            ((count, 2 * width), F32),
        ],
        [((width, n), BF16), ((n, 2 * width), BF16)],
    )

    x1 = exchange(stack((clusters, x0)), "gx", lambda i: i ^ 4)
    y1 = exchange(
        call(stack_after_border_kernel, (border, clusters, y0), ((BND + 2 * n, width), BF16)), "gy", lambda i: i ^ 3
    )
    z1 = exchange(stack((clusters, z0)), "gz", lambda i: i ^ 2)
    z2 = exchange(stack((clusters, z0, z1)), "gz", lambda i: i ^ 1)
    x2 = exchange(stack((clusters, x0, x1)), "gx", lambda i: i ^ 1)

    base = call(
        edge_kernel,
        (own, xa, xb, y0, y1, za, zb, weights, recv, base),
        ((count, width), F32),
        [((count + 6 * BND, width), F32), ((4, TILE, width), F32)],
        (senders.reshape(-1),),
    )
    line_y, top_x, acc_x, top_z, acc_z = call(
        middle_kernel,
        (own, weights, top, acc, y0, y1, x0, x1, z0, z1),
        [((count, width), F32)] + [((count, width), F32), ((count, 2 * width), F32)] * 2,
        [((width, 9 * n), BF16), ((9 * n, 2 * width), BF16)],
    )
    return call(
        final_kernel,
        (own, weights, gain, base, line_y, top_x, acc_x, top_z, acc_z, x2, z2),
        ((count, width), BF16),
        [((width, 8 * n), BF16), ((8 * n, 2 * width), BF16)],
        local=False,
    )


def solution(mesh):
    split = P(("gx", "gy", "gz"), None)
    in_specs = (split, split, split, P(("gx", "gy", "gz"))) + (P(),) * 7

    return jax.shard_map(on_device, mesh=mesh, in_specs=in_specs, out_specs=split, check_vma=False)
```

profile of v0, /device:TPU:1, one launch (start us, length us, event | category | flops | bytes accessed | tf_op | source)
XLA Modules:
  0.0 54.7 jit_solution(5106841725158538548)
XLA Ops:
  0.0 0.0 copy-start.7
  0.0 1.3 %load.1 = (bf16[1024,128]{1,0:T(8,128)(2,1)S(1)}, bf16[256,128]{1,0:T(8,128)(2,1)S(1)}, bf16[512,128]{1,0:T(8,128)(2,1)S(1)}, bf16[768,128]{1,0:T(8,128)(2,1)S(1...) custom-call(bf16[1024,128]{1,0:T(8,128)(2,1)} %own_far.1, bf16[256,128]{1,0:T(8,128)(2,1)} %clusters_far.1, ...), custom_call_target="tpu_custom_call" | custom-call | tf_op jit(solution)/shard_map/load/pallas_call | solution.py:255
  1.3 3.3 %collective-permute-start.2 = (bf16[768,128]{1,0:T(8,128)(2,1)S(1)}, bf16[768,128]{1,0:T(8,128)(2,1)S(1)}, u32[]{:S(2)}, u32[]{:S(2)}) collective-permute-start(bf16[768,128]{1,0:T(8,128)(2,1)S(1)} %get-tuple-element.27), channel_id=1, source_target_pairs={{0,8},{8,0},{16,24},{24,16},{1,9},{9,1},{17,25},{25,17},{2,10},{10... | collective-permute-start | bytes 589832 | tf_op jit(solution)/shard_map/ppermute | solution.py:227
  4.6 0.0 copy-done.7
  4.6 1.2 %collective-permute-start.6 = (bf16[256,128]{1,0:T(8,128)(2,1)S(1)}, bf16[256,128]{1,0:T(8,128)(2,1)S(1)}, u32[]{:S(2)}, u32[]{:S(2)}) collective-permute-start(bf16[256,128]{1,0:T(8,128)(2,1)S(1)} %copy-done.7), channel_id=1, source_target_pairs={{0,64},{32,96},{64,0},{96,32},{128,192},{160,224},{192,128},{224,1... | collective-permute-start | bytes 196616 | tf_op jit(solution)/shard_map/ppermute | solution.py:227
  5.8 6.9 %collective-permute-start.8 = (bf16[256,128]{1,0:T(8,128)(2,1)S(1)}, bf16[256,128]{1,0:T(8,128)(2,1)S(1)}, u32[]{:S(2)}, u32[]{:S(2)}) collective-permute-start(bf16[256,128]{1,0:T(8,128)(2,1)S(1)} %copy-done.7), channel_id=1, source_target_pairs={{0,4},{1,5},{2,6},{3,7},{4,0},{5,1},{6,2},{7,3},{8,12},{9,13},{10,... | collective-permute-start | bytes 196616 | tf_op jit(solution)/shard_map/ppermute | solution.py:227
  12.7 0.0 collective-permute-done.2.came.ya.y0
  12.7 1.9 %collective-permute-start.3 = (bf16[1024,128]{1,0:T(8,128)(2,1)S(1)}, bf16[1024,128]{1,0:T(8,128)(2,1)S(1)}, u32[]{:S(2)}, u32[]{:S(2)}) collective-permute-start(bf16[1024,128]{1,0:T(8,128)(2,1)S(1)} %shard_map.110), channel_id=1, source_target_pairs={{0,24},{8,16},{16,8},{24,0},{1,25},{9,17},{17,9},{25,1},{2,26},{10... | collective-permute-start | bytes 786440 | tf_op jit(solution)/shard_map/ppermute | solution.py:227
  14.6 0.0 collective-permute-done.6.refs_1_.x0
  14.6 2.5 %collective-permute-start.7 = (bf16[512,128]{1,0:T(8,128)(2,1)S(1)}, bf16[512,128]{1,0:T(8,128)(2,1)S(1)}, u32[]{:S(2)}, u32[]{:S(2)}) collective-permute-start(bf16[512,128]{1,0:T(8,128)(2,1)S(1)} %shard_map.112), channel_id=1, source_target_pairs={{0,128},{32,160},{64,192},{96,224},{128,0},{160,32},{192,64},{224,... | collective-permute-start | bytes 393224 | tf_op jit(solution)/shard_map/ppermute | solution.py:227
  17.1 0.0 collective-permute-done.8.refs_1_.z0
  17.1 1.3 %collective-permute-start.9 = (bf16[512,128]{1,0:T(8,128)(2,1)S(1)}, bf16[512,128]{1,0:T(8,128)(2,1)S(1)}, u32[]{:S(2)}, u32[]{:S(2)}) collective-permute-start(bf16[512,128]{1,0:T(8,128)(2,1)S(1)} %shard_map.113), channel_id=1, source_target_pairs={{0,2},{1,3},{2,0},{3,1},{4,6},{5,7},{6,4},{7,5},{8,10},{9,11},{10,... | collective-permute-start | bytes 393224 | tf_op jit(solution)/shard_map/ppermute | solution.py:227
  18.4 0.4 collective-permute-start
  18.8 7.8 %collective-permute-done.7.x1.refs_2_ = bf16[512,128]{1,0:T(8,128)(2,1)S(1)} collective-permute-done((bf16[512,128]{1,0:T(8,128)(2,1)S(1)}, bf16[512,128]{1,0:T(8,128)(2,1)S(1)}, u32[]{:S(2)}, u32[]{:S(2)}) %collective-permute-start.7) | collective-permute-done | bytes 131104 | tf_op jit(solution)/shard_map/ppermute | solution.py:227
  26.7 0.0 copy-start
  26.7 0.0 copy-start.1
  26.7 0.0 copy-start.2
  26.7 0.0 copy-start.3
  26.7 0.0 copy-start.4
  26.7 0.0 copy-start.5
  26.7 0.5 collective-permute-start.10
  27.2 0.0 collective-permute-done.9.z1.refs_2_
  27.3 0.8 %collective-permute-start.11 = (bf16[1024,128]{1,0:T(8,128)(2,1)S(1)}, bf16[1024,128]{1,0:T(8,128)(2,1)S(1)}, u32[]{:S(2)}, u32[]{:S(2)}) collective-permute-start(bf16[1024,128]{1,0:T(8,128)(2,1)S(1)} %shard_map.116), channel_id=1, source_target_pairs={{0,1},{1,0},{2,3},{3,2},{4,5},{5,4},{6,7},{7,6},{8,9},{9,8},{10,11... | collective-permute-start | bytes 786440 | tf_op jit(solution)/shard_map/ppermute | solution.py:227
  28.1 0.6 %collective-permute-start.1 = (bf16[512,128]{1,0:T(8,128)(2,1)S(1)}, bf16[512,128]{1,0:T(8,128)(2,1)S(1)}, u32[]{:S(2)}, u32[]{:S(2)}) collective-permute-start(bf16[512,128]{1,0:T(8,128)(2,1)S(1)} %get-tuple-element.26.border), channel_id=1, source_target_pairs={{0,224},{32,64},{64,32},{96,128},{128,96},{160,192},{192,160},{224... | collective-permute-start | bytes 393224 | tf_op jit(solution)/shard_map/ppermute | solution.py:227
  28.7 0.0 collective-permute-done.xa
  28.7 0.7 %collective-permute-start.4 = (bf16[512,128]{1,0:T(8,128)(2,1)S(1)}, bf16[512,128]{1,0:T(8,128)(2,1)S(1)}, u32[]{:S(2)}, u32[]{:S(2)}) collective-permute-start(bf16[512,128]{1,0:T(8,128)(2,1)S(1)} %get-tuple-element.26.border), channel_id=1, source_target_pairs={{0,1},{1,0},{2,3},{3,2},{4,5},{5,4},{6,7},{7,6},{8,9},{9,8},{10,11... | collective-permute-start | bytes 393224 | tf_op jit(solution)/shard_map/ppermute | solution.py:227
  29.5 0.0 collective-permute-done.3.yb.y1
  29.5 3.2 %collective-permute-start.5 = (bf16[512,128]{1,0:T(8,128)(2,1)S(1)}, bf16[512,128]{1,0:T(8,128)(2,1)S(1)}, u32[]{:S(2)}, u32[]{:S(2)}) collective-permute-start(bf16[512,128]{1,0:T(8,128)(2,1)S(1)} %get-tuple-element.26.border), channel_id=1, source_target_pairs={{0,7},{1,2},{2,1},{3,4},{4,3},{5,6},{6,5},{7,0},{8,15},{9,10},{10,... | collective-permute-start | bytes 393224 | tf_op jit(solution)/shard_map/ppermute | solution.py:227
  32.6 0.0 copy-done
  32.6 0.0 copy-done.1
  32.6 0.0 copy-done.2
  32.6 0.0 copy-done.3
  32.6 0.0 copy-done.4
  32.7 0.0 copy-done.5
  32.7 1.4 %shard_map.109 = (bf16[1280,128]{1,0:T(8,128)(2,1)S(1)}, f32[1024,128]{1,0:T(8,128)S(1)}, f32[1024,128]{1,0:T(8,128)S(1)}, f32[1024,128]{1,0:T(8,128)S(1)}, f32[1024,256]{1,0:T(8,128)S(1)}) custom-call(bf16[1024,128]{1,0:T(8,128)(2,1)S(1)} %get-tuple-element.21.own, bf16[256,128]{1,0:T(8,128)(2,1)S(1)} %get-tuple-element.22.clusters.refs_0_, ...), custom_call_target="tpu_custom_call" | custom-call | tf_op jit(solution)/shard_map/pallas_call | solution.py:215
  34.1 0.0 copy-start.6
  34.1 5.7 %shard_map.114 = (f32[1024,128]{1,0:T(8,128)S(1)}, f32[1024,128]{1,0:T(8,128)S(1)}, f32[1024,256]{1,0:T(8,128)S(1)}, f32[1024,128]{1,0:T(8,128)S(1)}, f32[1024,256]{1,0:T(8,128)S(1)}) custom-call(bf16[1024,128]{1,0:T(8,128)(2,1)S(1)} %get-tuple-element.21.own, bf16[1280,128]{1,0:T(8,128)(2,1)S(1)} %get-tuple-element.24.weights, ...), custom_call_target="tpu_custom_call" | custom-call | tf_op jit(solution)/shard_map/pallas_call | solution.py:215
  39.8 0.0 collective-permute-done.1.xb
  39.8 0.0 collective-permute-done.4.za
  39.8 0.0 collective-permute-done.5.zb
  39.8 0.0 copy-done.6
  39.8 7.3 %shard_map.111.base = f32[1024,128]{1,0:T(8,128)S(1)} custom-call(s32[4096]{0:T(1024)S(1)} %bitcast.3, bf16[1024,128]{1,0:T(8,128)(2,1)S(1)} %get-tuple-element.21.own, bf16[512,128]{1,0:T(8,128)(2,1)S(1)} %collective-permute-done.xa, bf16[512,128]{1,0:T(8,128)(2,1)S(1)} %collective-permute-done.1.xb, ...), custom_call_target="tpu_custom_call" | custom-call | tf_op jit(solution)/shard_map/pallas_call | solution.py:215
  47.1 0.0 collective-permute-done.10.x2
  47.1 0.0 collective-permute-done.11.z2
  47.1 7.6 %shard_map.117 = bf16[1024,128]{1,0:T(8,128)(2,1)} custom-call(bf16[1024,128]{1,0:T(8,128)(2,1)S(1)} %get-tuple-element.21.own, bf16[1280,128]{1,0:T(8,128)(2,1)S(1)} %get-tuple-element.24.weights, f32[1,128]{1,0:T(1,128)S(1)} %get-tuple-element.25.gain, f32[1024,128]{1,0:T(8,128)S(1)} %shard_map.111.base, f32[1024,128]{1,0:T(8,128)S(1)} %get-tuple-element.32.line_y, ...), custom_call_target="tpu_custom_call" | custom-call | tf_op jit(solution)/shard_map/pallas_call | solution.py:215
  (5 shorter events, 0.1 us)
Async XLA Ops:
  0.0 4.6 %copy-start.7 = (bf16[256,128]{1,0:T(8,128)(2,1)S(1)}, bf16[256,128]{1,0:T(8,128)(2,1)}, u32[]{:S(2)}) copy-start(bf16[256,128]{1,0:T(8,128)(2,1)} %clusters_far.1) | copy-start | bytes 196612
  1.3 11.4 %collective-permute-start.2 = (bf16[768,128]{1,0:T(8,128)(2,1)S(1)}, bf16[768,128]{1,0:T(8,128)(2,1)S(1)}, u32[]{:S(2)}, u32[]{:S(2)}) collective-permute-start(bf16[768,128]{1,0:T(8,128)(2,1)S(1)} %get-tuple-element.27), channel_id=1, source_target_pairs={{0,8},{8,0},{16,24},{24,16},{1,9},{9,1},{17,25},{25,17},{2,10},{10... | collective-permute-start | bytes 589832 | tf_op jit(solution)/shard_map/ppermute | solution.py:227
  4.6 10.0 %collective-permute-start.6 = (bf16[256,128]{1,0:T(8,128)(2,1)S(1)}, bf16[256,128]{1,0:T(8,128)(2,1)S(1)}, u32[]{:S(2)}, u32[]{:S(2)}) collective-permute-start(bf16[256,128]{1,0:T(8,128)(2,1)S(1)} %copy-done.7), channel_id=1, source_target_pairs={{0,64},{32,96},{64,0},{96,32},{128,192},{160,224},{192,128},{224,1... | collective-permute-start | bytes 196616 | tf_op jit(solution)/shard_map/ppermute | solution.py:227
  5.8 11.3 %collective-permute-start.8 = (bf16[256,128]{1,0:T(8,128)(2,1)S(1)}, bf16[256,128]{1,0:T(8,128)(2,1)S(1)}, u32[]{:S(2)}, u32[]{:S(2)}) collective-permute-start(bf16[256,128]{1,0:T(8,128)(2,1)S(1)} %copy-done.7), channel_id=1, source_target_pairs={{0,4},{1,5},{2,6},{3,7},{4,0},{5,1},{6,2},{7,3},{8,12},{9,13},{10,... | collective-permute-start | bytes 196616 | tf_op jit(solution)/shard_map/ppermute | solution.py:227
  12.7 16.8 %collective-permute-start.3 = (bf16[1024,128]{1,0:T(8,128)(2,1)S(1)}, bf16[1024,128]{1,0:T(8,128)(2,1)S(1)}, u32[]{:S(2)}, u32[]{:S(2)}) collective-permute-start(bf16[1024,128]{1,0:T(8,128)(2,1)S(1)} %shard_map.110), channel_id=1, source_target_pairs={{0,24},{8,16},{16,8},{24,0},{1,25},{9,17},{17,9},{25,1},{2,26},{10... | collective-permute-start | bytes 786440 | tf_op jit(solution)/shard_map/ppermute | solution.py:227
  14.6 12.1 %collective-permute-start.7 = (bf16[512,128]{1,0:T(8,128)(2,1)S(1)}, bf16[512,128]{1,0:T(8,128)(2,1)S(1)}, u32[]{:S(2)}, u32[]{:S(2)}) collective-permute-start(bf16[512,128]{1,0:T(8,128)(2,1)S(1)} %shard_map.112), channel_id=1, source_target_pairs={{0,128},{32,160},{64,192},{96,224},{128,0},{160,32},{192,64},{224,... | collective-permute-start | bytes 393224 | tf_op jit(solution)/shard_map/ppermute | solution.py:227
  17.1 10.1 %collective-permute-start.9 = (bf16[512,128]{1,0:T(8,128)(2,1)S(1)}, bf16[512,128]{1,0:T(8,128)(2,1)S(1)}, u32[]{:S(2)}, u32[]{:S(2)}) collective-permute-start(bf16[512,128]{1,0:T(8,128)(2,1)S(1)} %shard_map.113), channel_id=1, source_target_pairs={{0,2},{1,3},{2,0},{3,1},{4,6},{5,7},{6,4},{7,5},{8,10},{9,11},{10,... | collective-permute-start | bytes 393224 | tf_op jit(solution)/shard_map/ppermute | solution.py:227
  18.4 10.3 %collective-permute-start = (bf16[512,128]{1,0:T(8,128)(2,1)S(1)}, bf16[512,128]{1,0:T(8,128)(2,1)S(1)}, u32[]{:S(2)}, u32[]{:S(2)}) collective-permute-start(bf16[512,128]{1,0:T(8,128)(2,1)S(1)} %get-tuple-element.26.border), channel_id=1, source_target_pairs={{0,32},{32,0},{64,96},{96,64},{128,160},{160,128},{192,224},{224,1... | collective-permute-start | bytes 393224 | tf_op jit(solution)/shard_map/ppermute | solution.py:227
  26.7 6.0 %copy-start = (bf16[512,128]{1,0:T(8,128)(2,1)S(1)}, bf16[512,128]{1,0:T(8,128)(2,1)}, u32[]{:S(2)}) copy-start(bf16[512,128]{1,0:T(8,128)(2,1)} %w_node.1) | copy-start | bytes 393220
  26.7 6.0 %copy-start.1 = (bf16[256,128]{1,0:T(8,128)(2,1)S(1)}, bf16[256,128]{1,0:T(8,128)(2,1)}, u32[]{:S(2)}) copy-start(bf16[256,128]{1,0:T(8,128)(2,1)} %w_in.1) | copy-start | bytes 196612
  26.7 5.9 %copy-start.2 = (bf16[128,128]{1,0:T(8,128)(2,1)S(1)}, bf16[128,128]{1,0:T(8,128)(2,1)}, u32[]{:S(2)}) copy-start(bf16[128,128]{1,0:T(8,128)(2,1)} %w_key.1) | copy-start | bytes 98308
  26.7 5.9 %copy-start.3 = (bf16[128,128]{1,0:T(8,128)(2,1)S(1)}, bf16[128,128]{1,0:T(8,128)(2,1)}, u32[]{:S(2)}) copy-start(bf16[128,128]{1,0:T(8,128)(2,1)} %w_value.1) | copy-start | bytes 98308
  26.7 5.9 %copy-start.4 = (bf16[128,128]{1,0:T(8,128)(2,1)S(1)}, bf16[128,128]{1,0:T(8,128)(2,1)}, u32[]{:S(2)}) copy-start(bf16[128,128]{1,0:T(8,128)(2,1)} %w_msg.1) | copy-start | bytes 98308
  26.7 5.9 %copy-start.5 = (bf16[128,128]{1,0:T(8,128)(2,1)S(1)}, bf16[128,128]{1,0:T(8,128)(2,1)}, u32[]{:S(2)}) copy-start(bf16[128,128]{1,0:T(8,128)(2,1)} %w_out.1) | copy-start | bytes 98308
  26.7 20.3 %collective-permute-start.10 = (bf16[1024,128]{1,0:T(8,128)(2,1)S(1)}, bf16[1024,128]{1,0:T(8,128)(2,1)S(1)}, u32[]{:S(2)}, u32[]{:S(2)}) collective-permute-start(bf16[1024,128]{1,0:T(8,128)(2,1)S(1)} %shard_map.115), channel_id=1, source_target_pairs={{0,32},{32,0},{64,96},{96,64},{128,160},{160,128},{192,224},{224,1... | collective-permute-start | bytes 786440 | tf_op jit(solution)/shard_map/ppermute | solution.py:227
  27.3 19.8 %collective-permute-start.11 = (bf16[1024,128]{1,0:T(8,128)(2,1)S(1)}, bf16[1024,128]{1,0:T(8,128)(2,1)S(1)}, u32[]{:S(2)}, u32[]{:S(2)}) collective-permute-start(bf16[1024,128]{1,0:T(8,128)(2,1)S(1)} %shard_map.116), channel_id=1, source_target_pairs={{0,1},{1,0},{2,3},{3,2},{4,5},{5,4},{6,7},{7,6},{8,9},{9,8},{10,11... | collective-permute-start | bytes 786440 | tf_op jit(solution)/shard_map/ppermute | solution.py:227
  28.1 11.7 %collective-permute-start.1 = (bf16[512,128]{1,0:T(8,128)(2,1)S(1)}, bf16[512,128]{1,0:T(8,128)(2,1)S(1)}, u32[]{:S(2)}, u32[]{:S(2)}) collective-permute-start(bf16[512,128]{1,0:T(8,128)(2,1)S(1)} %get-tuple-element.26.border), channel_id=1, source_target_pairs={{0,224},{32,64},{64,32},{96,128},{128,96},{160,192},{192,160},{224... | collective-permute-start | bytes 393224 | tf_op jit(solution)/shard_map/ppermute | solution.py:227
  28.7 11.1 %collective-permute-start.4 = (bf16[512,128]{1,0:T(8,128)(2,1)S(1)}, bf16[512,128]{1,0:T(8,128)(2,1)S(1)}, u32[]{:S(2)}, u32[]{:S(2)}) collective-permute-start(bf16[512,128]{1,0:T(8,128)(2,1)S(1)} %get-tuple-element.26.border), channel_id=1, source_target_pairs={{0,1},{1,0},{2,3},{3,2},{4,5},{5,4},{6,7},{7,6},{8,9},{9,8},{10,11... | collective-permute-start | bytes 393224 | tf_op jit(solution)/shard_map/ppermute | solution.py:227
  29.5 10.3 %collective-permute-start.5 = (bf16[512,128]{1,0:T(8,128)(2,1)S(1)}, bf16[512,128]{1,0:T(8,128)(2,1)S(1)}, u32[]{:S(2)}, u32[]{:S(2)}) collective-permute-start(bf16[512,128]{1,0:T(8,128)(2,1)S(1)} %get-tuple-element.26.border), channel_id=1, source_target_pairs={{0,7},{1,2},{2,1},{3,4},{4,3},{5,6},{6,5},{7,0},{8,15},{9,10},{10,... | collective-permute-start | bytes 393224 | tf_op jit(solution)/shard_map/ppermute | solution.py:227
  34.1 5.7 %copy-start.6 = (s32[32,128]{1,0:T(8,128)S(1)}, s32[32,128]{1,0:T(8,128)}, u32[]{:S(2)}) copy-start(s32[32,128]{1,0:T(8,128)} %param.13) | copy-start | bytes 49156
where the time goes:
time: 54.7 us
  starting transfers between devices  23.3 us (43%)
  Pallas kernels  23.2 us (42%)
  waiting for transfers between devices  7.88 us (14%)
    ppermute x12, starting transfers between devices, exchange(): return lax.ppermute(x, axis, [(i, partner(i) % size) for i in range(size)])  23.3 us
    pallas_call x9, Pallas kernels, call(): pl.pallas_call(kernel, out_shape=[space(*o) for o in outs] if many else s...  22 us
    ppermute x12, waiting for transfers between devices, exchange(): return lax.ppermute(x, axis, [(i, partner(i) % size) for i in range(size)])  7.88 us
    pallas_call x1, Pallas kernels, on_device(): pl.pallas_call(load_kernel, out_shape=[pltpu.VMEM((count, width), BF16),...  1.26 us
  transfers between devices with their start and end apart: 12, of which 1 were waited for; matrix products, arithmetic and copies ran while one was open for 0% of the time, Pallas kernels for 26%

commit v1 on v0

--- a/solution.py
+++ b/solution.py
@@ -13,6 +13,7 @@
 BF16 = jnp.bfloat16
 TILE = 128
 ROWS = 256
+NODES_STEP = 64
 VMEM_BYTES = 20 * 2**20
 
 VMEM = pl.BlockSpec(memory_space=pltpu.VMEM)
@@ -42,12 +43,8 @@
     return math.log2(math.e) / math.sqrt(width)
 
 
-def row_loop(count, body):
-    def step(r, _):
-        body(pl.ds(pl.multiple_of(r * ROWS, ROWS), ROWS))
-        return 0
-
-    lax.fori_loop(0, count // ROWS, step, 0)
+def row_tiles(count, rows):
+    return [pl.ds(at, rows) for at in range(0, count, rows)]
 
 
 def project(pieces, weights, keys, values):
@@ -151,23 +148,18 @@
         table[pl.ds(high, BND), :] = dot(pair[1][:BND, :], w_send)
     w_sum = jnp.concatenate([weight(weights, W_MSG)] * 4, axis=0)
 
-    def tile(t, _):
-        def gather(g, _):
-            for j in range(16):
-                for d in range(4):
-                    index = senders[t * TILE * 4 + g * 64 + j * 4 + d]
-                    rows[d, pl.ds(pl.multiple_of(g * 16, 16) + j, 1), :] = table[pl.ds(index, 1), :]
-            return 0
-
-        lax.fori_loop(0, TILE // 16, gather, 0)
-        here = pl.ds(pl.multiple_of(t * TILE, TILE), TILE)
-        r = recv[here, :]
-        hidden = jnp.concatenate([silu(rows[d] + r).astype(BF16) for d in range(4)], axis=1)
-        agg = dot(hidden, w_sum).astype(BF16)
-        out[here, :] = base[here, :] + dot(agg, weight(weights, W_AGG))
+    def gather(g, _):
+        for j in range(NODES_STEP):
+            for d in range(4):
+                index = senders[g * NODES_STEP * 4 + j * 4 + d]
+                at = pl.multiple_of(g * NODES_STEP, NODES_STEP) + j
+                rows[d, pl.ds(at, 1), :] = table[pl.ds(index, 1), :]
         return 0
 
-    lax.fori_loop(0, count // TILE, tile, 0)
+    lax.fori_loop(0, count // NODES_STEP, gather, 0)
+    hidden = jnp.concatenate([silu(rows[d] + recv[...]).astype(BF16) for d in range(4)], axis=1)
+    agg = dot(hidden, w_sum).astype(BF16)
+    out[...] = base[...] + dot(agg, weight(weights, W_AGG))
 
 
 def middle_kernel(own, weights, top0, acc0, y0, y1, x0, x1, z0, z1, line_y, top_x, acc_x, top_z, acc_z, keys, values):
@@ -175,7 +167,7 @@
     n = x0.shape[0]
     project((y0.at[BND:, :], y1.at[BND:, :], x0, x1, z0, z1), weights, keys, values)
 
-    def rows(here):
+    for here in row_tiles(count, ROWS):
         q = own[here, :]
         t0, a0 = top0[here, :], acc0[here, :]
         _, a = absorb(q, keys[:, 0 : 3 * n], values[0 : 3 * n, :], t0, a0)
@@ -183,30 +175,29 @@
         top_x[here, :], acc_x[here, :] = absorb(q, keys[:, 3 * n : 6 * n], values[3 * n : 6 * n, :], t0, a0)
         top_z[here, :], acc_z[here, :] = absorb(q, keys[:, 6 * n : 9 * n], values[6 * n : 9 * n, :], t0, a0)
 
-    row_loop(count, rows)
-
-
-def final_kernel(own, weights, gain, base, line_y, top_x, acc_x, top_z, acc_z, x2, z2, out, keys, values):
+
+def final_kernel(
+    own, weights, gain, base, line_y, top_x, acc_x, top_z, acc_z, x2, z2, out, keys, values, pooled
+):
     count, width = own.shape
     n = x2.shape[0]
     project((x2, z2), weights, keys, values)
-
-    def rows(here):
+    for here in row_tiles(count, ROWS):
         q = own[here, :]
         _, ax = absorb(q, keys[:, 0:n], values[0:n, :], top_x[here, :], acc_x[here, :])
         _, az = absorb(q, keys[:, n : 2 * n], values[n : 2 * n, :], top_z[here, :], acc_z[here, :])
-        pooled = line_y[here, :] + ax[:, :width] / ax[:, width:] + az[:, :width] / az[:, width:]
-        attended = (
-            pooled * lax.rsqrt(jnp.mean(pooled * pooled, axis=1, keepdims=True) + 1e-06)
-        ).astype(BF16)
+        pooled[here, :] = (
+            line_y[here, :] + ax[:, :width] / ax[:, width:] + az[:, :width] / az[:, width:]
+        )
+    for here in row_tiles(count, 2 * ROWS):
+        p = pooled[here, :]
+        attended = (p * lax.rsqrt(jnp.mean(p * p, axis=1, keepdims=True) + 1e-06)).astype(BF16)
         preact = base[here, :] + dot(attended, weight(weights, W_ATT))
         update = dot(silu(preact).astype(BF16), weight(weights, W_OUT))
         centred = update - jnp.mean(update, axis=1, keepdims=True)
         variance = jnp.mean(centred * centred, axis=1, keepdims=True)
         normed = centred * lax.rsqrt(variance + 1e-05)
-        out[here, :] = (q.astype(F32) + normed * gain[...]).astype(BF16)
-
-    row_loop(count, rows)
+        out[here, :] = (own[here, :].astype(F32) + normed * gain[...]).astype(BF16)
 
 
 def call(kernel, args, outs, scratch=(), scalars=(), local=True):
@@ -309,7 +300,9 @@
 
     x1 = exchange(stack((clusters, x0)), "gx", lambda i: i ^ 4)
     y1 = exchange(
-        call(stack_after_border_kernel, (border, clusters, y0), ((BND + 2 * n, width), BF16)), "gy", lambda i: i ^ 3
+        call(stack_after_border_kernel, (border, clusters, y0), ((BND + 2 * n, width), BF16)),
+        "gy",
+        lambda i: i ^ 3,
     )
     z1 = exchange(stack((clusters, z0)), "gz", lambda i: i ^ 2)
     z2 = exchange(stack((clusters, z0, z1)), "gz", lambda i: i ^ 1)
@@ -319,7 +312,7 @@
         edge_kernel,
         (own, xa, xb, y0, y1, za, zb, weights, recv, base),
         ((count, width), F32),
-        [((count + 6 * BND, width), F32), ((4, TILE, width), F32)],
+        [((count + 6 * BND, width), F32), ((4, count, width), F32)],
         (senders.reshape(-1),),
     )
     line_y, top_x, acc_x, top_z, acc_z = call(
@@ -332,7 +325,7 @@
         final_kernel,
         (own, weights, gain, base, line_y, top_x, acc_x, top_z, acc_z, x2, z2),
         ((count, width), BF16),
-        [((width, 8 * n), BF16), ((8 * n, 2 * width), BF16)],
+        [((width, 8 * n), BF16), ((8 * n, 2 * width), BF16), ((count, width), F32)],
         local=False,
     )
 

time: 54.7 us -> 47.7 us (0.87)
  Pallas kernels: 23.2 us -> 16.2 us
    pallas_call x9, Pallas kernels: 22 us -> 14.9 us  [call(): pl.pallas_call(kernel, out_shape=[space(*o) for o in outs] if many else s...]
  transfers between devices with their start and end apart: 12 -> 12, of which waited for: 1 -> 1; matrix products, arithmetic and copies ran while one was open for 0% -> 0% of each run, Pallas kernels for 26% -> 22%
where the time goes in v1:
time: 47.7 us; the launch traced here: 47.6 us
  starting transfers between devices  23.3 us (49%)
  Pallas kernels  16.2 us (34%)
  waiting for transfers between devices  7.88 us (17%)
    ppermute x12, starting transfers between devices, exchange(): return lax.ppermute(x, axis, [(i, partner(i) % size) for i in range(size)])  23.3 us
    pallas_call x9, Pallas kernels, call(): pl.pallas_call(kernel, out_shape=[space(*o) for o in outs] if many else s...  14.9 us
    ppermute x12, waiting for transfers between devices, exchange(): return lax.ppermute(x, axis, [(i, partner(i) % size) for i in range(size)])  7.88 us
    pallas_call x1, Pallas kernels, on_device(): pl.pallas_call(load_kernel, out_shape=[pltpu.VMEM((count, width), BF16),...  1.26 us
  transfers between devices with their start and end apart: 12, of which 1 were waited for; matrix products, arithmetic and copies ran while one was open for 0% of the time, Pallas kernels for 22%

profile of v1, /device:TPU:1, one launch (start us, length us, event | category | flops | bytes accessed | tf_op | source)
XLA Modules:
  0.0 47.6 jit_solution(1467184056065024313)
XLA Ops:
  0.0 0.0 copy-start.7
  0.0 1.3 %load.1 = (bf16[1024,128]{1,0:T(8,128)(2,1)S(1)}, bf16[256,128]{1,0:T(8,128)(2,1)S(1)}, bf16[512,128]{1,0:T(8,128)(2,1)S(1)}, bf16[768,128]{1,0:T(8,128)(2,1)S(1...) custom-call(bf16[1024,128]{1,0:T(8,128)(2,1)} %own_far.1, bf16[256,128]{1,0:T(8,128)(2,1)} %clusters_far.1, ...), custom_call_target="tpu_custom_call" | custom-call | tf_op jit(solution)/shard_map/load/pallas_call | solution.py:246
  1.3 3.3 %collective-permute-start.2 = (bf16[768,128]{1,0:T(8,128)(2,1)S(1)}, bf16[768,128]{1,0:T(8,128)(2,1)S(1)}, u32[]{:S(2)}, u32[]{:S(2)}) collective-permute-start(bf16[768,128]{1,0:T(8,128)(2,1)S(1)} %get-tuple-element.27), channel_id=1, source_target_pairs={{0,8},{8,0},{16,24},{24,16},{1,9},{9,1},{17,25},{25,17},{2,10},{10... | collective-permute-start | bytes 589832 | tf_op jit(solution)/shard_map/ppermute | solution.py:218
  4.6 0.0 copy-done.7
  4.6 1.2 %collective-permute-start.6 = (bf16[256,128]{1,0:T(8,128)(2,1)S(1)}, bf16[256,128]{1,0:T(8,128)(2,1)S(1)}, u32[]{:S(2)}, u32[]{:S(2)}) collective-permute-start(bf16[256,128]{1,0:T(8,128)(2,1)S(1)} %copy-done.7), channel_id=1, source_target_pairs={{0,64},{32,96},{64,0},{96,32},{128,192},{160,224},{192,128},{224,1... | collective-permute-start | bytes 196616 | tf_op jit(solution)/shard_map/ppermute | solution.py:218
  5.8 6.9 %collective-permute-start.8 = (bf16[256,128]{1,0:T(8,128)(2,1)S(1)}, bf16[256,128]{1,0:T(8,128)(2,1)S(1)}, u32[]{:S(2)}, u32[]{:S(2)}) collective-permute-start(bf16[256,128]{1,0:T(8,128)(2,1)S(1)} %copy-done.7), channel_id=1, source_target_pairs={{0,4},{1,5},{2,6},{3,7},{4,0},{5,1},{6,2},{7,3},{8,12},{9,13},{10,... | collective-permute-start | bytes 196616 | tf_op jit(solution)/shard_map/ppermute | solution.py:218
  12.7 0.0 collective-permute-done.2.came.ya.y0
  12.7 1.9 %collective-permute-start.3 = (bf16[1024,128]{1,0:T(8,128)(2,1)S(1)}, bf16[1024,128]{1,0:T(8,128)(2,1)S(1)}, u32[]{:S(2)}, u32[]{:S(2)}) collective-permute-start(bf16[1024,128]{1,0:T(8,128)(2,1)S(1)} %shard_map.110), channel_id=1, source_target_pairs={{0,24},{8,16},{16,8},{24,0},{1,25},{9,17},{17,9},{25,1},{2,26},{10... | collective-permute-start | bytes 786440 | tf_op jit(solution)/shard_map/ppermute | solution.py:218
  14.6 0.0 collective-permute-done.6.refs_1_.x0
  14.6 2.5 %collective-permute-start.7 = (bf16[512,128]{1,0:T(8,128)(2,1)S(1)}, bf16[512,128]{1,0:T(8,128)(2,1)S(1)}, u32[]{:S(2)}, u32[]{:S(2)}) collective-permute-start(bf16[512,128]{1,0:T(8,128)(2,1)S(1)} %shard_map.112), channel_id=1, source_target_pairs={{0,128},{32,160},{64,192},{96,224},{128,0},{160,32},{192,64},{224,... | collective-permute-start | bytes 393224 | tf_op jit(solution)/shard_map/ppermute | solution.py:218
  17.1 0.0 collective-permute-done.8.refs_1_.z0
  17.1 1.3 %collective-permute-start.9 = (bf16[512,128]{1,0:T(8,128)(2,1)S(1)}, bf16[512,128]{1,0:T(8,128)(2,1)S(1)}, u32[]{:S(2)}, u32[]{:S(2)}) collective-permute-start(bf16[512,128]{1,0:T(8,128)(2,1)S(1)} %shard_map.113), channel_id=1, source_target_pairs={{0,2},{1,3},{2,0},{3,1},{4,6},{5,7},{6,4},{7,5},{8,10},{9,11},{10,... | collective-permute-start | bytes 393224 | tf_op jit(solution)/shard_map/ppermute | solution.py:218
  18.4 0.4 collective-permute-start
  18.8 7.8 %collective-permute-done.7.x1.refs_2_ = bf16[512,128]{1,0:T(8,128)(2,1)S(1)} collective-permute-done((bf16[512,128]{1,0:T(8,128)(2,1)S(1)}, bf16[512,128]{1,0:T(8,128)(2,1)S(1)}, u32[]{:S(2)}, u32[]{:S(2)}) %collective-permute-start.7) | collective-permute-done | bytes 131104 | tf_op jit(solution)/shard_map/ppermute | solution.py:218
  26.7 0.0 copy-start
  26.7 0.0 copy-start.1
  26.7 0.0 copy-start.2
  26.7 0.0 copy-start.3
  26.7 0.0 copy-start.4
  26.7 0.0 copy-start.5
  26.7 0.5 %collective-permute-start.10 = (bf16[1024,128]{1,0:T(8,128)(2,1)S(1)}, bf16[1024,128]{1,0:T(8,128)(2,1)S(1)}, u32[]{:S(2)}, u32[]{:S(2)}) collective-permute-start(bf16[1024,128]{1,0:T(8,128)(2,1)S(1)} %shard_map.115), channel_id=1, source_target_pairs={{0,32},{32,0},{64,96},{96,64},{128,160},{160,128},{192,224},{224,1... | collective-permute-start | bytes 786440 | tf_op jit(solution)/shard_map/ppermute | solution.py:218
  27.2 0.0 collective-permute-done.9.z1.refs_2_
  27.3 0.8 %collective-permute-start.11 = (bf16[1024,128]{1,0:T(8,128)(2,1)S(1)}, bf16[1024,128]{1,0:T(8,128)(2,1)S(1)}, u32[]{:S(2)}, u32[]{:S(2)}) collective-permute-start(bf16[1024,128]{1,0:T(8,128)(2,1)S(1)} %shard_map.116), channel_id=1, source_target_pairs={{0,1},{1,0},{2,3},{3,2},{4,5},{5,4},{6,7},{7,6},{8,9},{9,8},{10,11... | collective-permute-start | bytes 786440 | tf_op jit(solution)/shard_map/ppermute | solution.py:218
  28.1 0.6 %collective-permute-start.1 = (bf16[512,128]{1,0:T(8,128)(2,1)S(1)}, bf16[512,128]{1,0:T(8,128)(2,1)S(1)}, u32[]{:S(2)}, u32[]{:S(2)}) collective-permute-start(bf16[512,128]{1,0:T(8,128)(2,1)S(1)} %get-tuple-element.26.border), channel_id=1, source_target_pairs={{0,224},{32,64},{64,32},{96,128},{128,96},{160,192},{192,160},{224... | collective-permute-start | bytes 393224 | tf_op jit(solution)/shard_map/ppermute | solution.py:218
  28.7 0.0 collective-permute-done.xa
  28.7 0.7 %collective-permute-start.4 = (bf16[512,128]{1,0:T(8,128)(2,1)S(1)}, bf16[512,128]{1,0:T(8,128)(2,1)S(1)}, u32[]{:S(2)}, u32[]{:S(2)}) collective-permute-start(bf16[512,128]{1,0:T(8,128)(2,1)S(1)} %get-tuple-element.26.border), channel_id=1, source_target_pairs={{0,1},{1,0},{2,3},{3,2},{4,5},{5,4},{6,7},{7,6},{8,9},{9,8},{10,11... | collective-permute-start | bytes 393224 | tf_op jit(solution)/shard_map/ppermute | solution.py:218
  29.5 0.0 collective-permute-done.3.yb.y1
  29.5 3.2 %collective-permute-start.5 = (bf16[512,128]{1,0:T(8,128)(2,1)S(1)}, bf16[512,128]{1,0:T(8,128)(2,1)S(1)}, u32[]{:S(2)}, u32[]{:S(2)}) collective-permute-start(bf16[512,128]{1,0:T(8,128)(2,1)S(1)} %get-tuple-element.26.border), channel_id=1, source_target_pairs={{0,7},{1,2},{2,1},{3,4},{4,3},{5,6},{6,5},{7,0},{8,15},{9,10},{10,... | collective-permute-start | bytes 393224 | tf_op jit(solution)/shard_map/ppermute | solution.py:218
  32.6 0.0 copy-done
  32.6 0.0 copy-done.1
  32.6 0.0 copy-done.2
  32.6 0.0 copy-done.3
  32.6 0.0 copy-done.4
  32.7 0.0 copy-done.5
  32.7 1.4 %shard_map.109 = (bf16[1280,128]{1,0:T(8,128)(2,1)S(1)}, f32[1024,128]{1,0:T(8,128)S(1)}, f32[1024,128]{1,0:T(8,128)S(1)}, f32[1024,128]{1,0:T(8,128)S(1)}, f32[1024,256]{1,0:T(8,128)S(1)}) custom-call(bf16[1024,128]{1,0:T(8,128)(2,1)S(1)} %get-tuple-element.21.own, bf16[256,128]{1,0:T(8,128)(2,1)S(1)} %get-tuple-element.22.clusters.refs_0_, ...), custom_call_target="tpu_custom_call" | custom-call | tf_op jit(solution)/shard_map/pallas_call | solution.py:206
  34.1 0.0 copy-start.6
  34.1 3.7 %shard_map.114 = (f32[1024,128]{1,0:T(8,128)S(1)}, f32[1024,128]{1,0:T(8,128)S(1)}, f32[1024,256]{1,0:T(8,128)S(1)}, f32[1024,128]{1,0:T(8,128)S(1)}, f32[1024,256]{1,0:T(8,128)S(1)}) custom-call(bf16[1024,128]{1,0:T(8,128)(2,1)S(1)} %get-tuple-element.21.own, bf16[1280,128]{1,0:T(8,128)(2,1)S(1)} %get-tuple-element.24.weights, ...), custom_call_target="tpu_custom_call" | custom-call | tf_op jit(solution)/shard_map/pallas_call | solution.py:206
  37.8 0.0 collective-permute-done.1.xb
  37.8 0.0 collective-permute-done.4.za
  37.8 0.0 collective-permute-done.5.zb
  37.8 0.0 copy-done.6
  37.9 5.3 %shard_map.111.base = f32[1024,128]{1,0:T(8,128)S(1)} custom-call(s32[4096]{0:T(1024)S(1)} %bitcast.3, bf16[1024,128]{1,0:T(8,128)(2,1)S(1)} %get-tuple-element.21.own, bf16[512,128]{1,0:T(8,128)(2,1)S(1)} %collective-permute-done.xa, bf16[512,128]{1,0:T(8,128)(2,1)S(1)} %collective-permute-done.1.xb, ...), custom_call_target="tpu_custom_call" | custom-call | tf_op jit(solution)/shard_map/pallas_call | solution.py:206
  43.1 0.0 collective-permute-done.10.x2
  43.1 0.0 collective-permute-done.11.z2
  43.1 4.4 %shard_map.117 = bf16[1024,128]{1,0:T(8,128)(2,1)} custom-call(bf16[1024,128]{1,0:T(8,128)(2,1)S(1)} %get-tuple-element.21.own, bf16[1280,128]{1,0:T(8,128)(2,1)S(1)} %get-tuple-element.24.weights, f32[1,128]{1,0:T(1,128)S(1)} %get-tuple-element.25.gain, f32[1024,128]{1,0:T(8,128)S(1)} %shard_map.111.base, f32[1024,128]{1,0:T(8,128)S(1)} %get-tuple-element.32.line_y, ...), custom_call_target="tpu_custom_call" | custom-call | tf_op jit(solution)/shard_map/pallas_call | solution.py:206
  (5 shorter events, 0.1 us)
Async XLA Ops:
  0.0 4.6 %copy-start.7 = (bf16[256,128]{1,0:T(8,128)(2,1)S(1)}, bf16[256,128]{1,0:T(8,128)(2,1)}, u32[]{:S(2)}) copy-start(bf16[256,128]{1,0:T(8,128)(2,1)} %clusters_far.1) | copy-start | bytes 196612
  1.3 11.4 %collective-permute-start.2 = (bf16[768,128]{1,0:T(8,128)(2,1)S(1)}, bf16[768,128]{1,0:T(8,128)(2,1)S(1)}, u32[]{:S(2)}, u32[]{:S(2)}) collective-permute-start(bf16[768,128]{1,0:T(8,128)(2,1)S(1)} %get-tuple-element.27), channel_id=1, source_target_pairs={{0,8},{8,0},{16,24},{24,16},{1,9},{9,1},{17,25},{25,17},{2,10},{10... | collective-permute-start | bytes 589832 | tf_op jit(solution)/shard_map/ppermute | solution.py:218
  4.6 10.0 %collective-permute-start.6 = (bf16[256,128]{1,0:T(8,128)(2,1)S(1)}, bf16[256,128]{1,0:T(8,128)(2,1)S(1)}, u32[]{:S(2)}, u32[]{:S(2)}) collective-permute-start(bf16[256,128]{1,0:T(8,128)(2,1)S(1)} %copy-done.7), channel_id=1, source_target_pairs={{0,64},{32,96},{64,0},{96,32},{128,192},{160,224},{192,128},{224,1... | collective-permute-start | bytes 196616 | tf_op jit(solution)/shard_map/ppermute | solution.py:218
  5.8 11.3 %collective-permute-start.8 = (bf16[256,128]{1,0:T(8,128)(2,1)S(1)}, bf16[256,128]{1,0:T(8,128)(2,1)S(1)}, u32[]{:S(2)}, u32[]{:S(2)}) collective-permute-start(bf16[256,128]{1,0:T(8,128)(2,1)S(1)} %copy-done.7), channel_id=1, source_target_pairs={{0,4},{1,5},{2,6},{3,7},{4,0},{5,1},{6,2},{7,3},{8,12},{9,13},{10,... | collective-permute-start | bytes 196616 | tf_op jit(solution)/shard_map/ppermute | solution.py:218
  12.7 16.8 %collective-permute-start.3 = (bf16[1024,128]{1,0:T(8,128)(2,1)S(1)}, bf16[1024,128]{1,0:T(8,128)(2,1)S(1)}, u32[]{:S(2)}, u32[]{:S(2)}) collective-permute-start(bf16[1024,128]{1,0:T(8,128)(2,1)S(1)} %shard_map.110), channel_id=1, source_target_pairs={{0,24},{8,16},{16,8},{24,0},{1,25},{9,17},{17,9},{25,1},{2,26},{10... | collective-permute-start | bytes 786440 | tf_op jit(solution)/shard_map/ppermute | solution.py:218
  14.6 12.1 %collective-permute-start.7 = (bf16[512,128]{1,0:T(8,128)(2,1)S(1)}, bf16[512,128]{1,0:T(8,128)(2,1)S(1)}, u32[]{:S(2)}, u32[]{:S(2)}) collective-permute-start(bf16[512,128]{1,0:T(8,128)(2,1)S(1)} %shard_map.112), channel_id=1, source_target_pairs={{0,128},{32,160},{64,192},{96,224},{128,0},{160,32},{192,64},{224,... | collective-permute-start | bytes 393224 | tf_op jit(solution)/shard_map/ppermute | solution.py:218
  17.1 10.1 %collective-permute-start.9 = (bf16[512,128]{1,0:T(8,128)(2,1)S(1)}, bf16[512,128]{1,0:T(8,128)(2,1)S(1)}, u32[]{:S(2)}, u32[]{:S(2)}) collective-permute-start(bf16[512,128]{1,0:T(8,128)(2,1)S(1)} %shard_map.113), channel_id=1, source_target_pairs={{0,2},{1,3},{2,0},{3,1},{4,6},{5,7},{6,4},{7,5},{8,10},{9,11},{10,... | collective-permute-start | bytes 393224 | tf_op jit(solution)/shard_map/ppermute | solution.py:218
  18.4 10.3 %collective-permute-start = (bf16[512,128]{1,0:T(8,128)(2,1)S(1)}, bf16[512,128]{1,0:T(8,128)(2,1)S(1)}, u32[]{:S(2)}, u32[]{:S(2)}) collective-permute-start(bf16[512,128]{1,0:T(8,128)(2,1)S(1)} %get-tuple-element.26.border), channel_id=1, source_target_pairs={{0,32},{32,0},{64,96},{96,64},{128,160},{160,128},{192,224},{224,1... | collective-permute-start | bytes 393224 | tf_op jit(solution)/shard_map/ppermute | solution.py:218
  26.7 6.0 %copy-start = (bf16[512,128]{1,0:T(8,128)(2,1)S(1)}, bf16[512,128]{1,0:T(8,128)(2,1)}, u32[]{:S(2)}) copy-start(bf16[512,128]{1,0:T(8,128)(2,1)} %w_node.1) | copy-start | bytes 393220
  26.7 6.0 %copy-start.1 = (bf16[256,128]{1,0:T(8,128)(2,1)S(1)}, bf16[256,128]{1,0:T(8,128)(2,1)}, u32[]{:S(2)}) copy-start(bf16[256,128]{1,0:T(8,128)(2,1)} %w_in.1) | copy-start | bytes 196612
  26.7 5.9 %copy-start.2 = (bf16[128,128]{1,0:T(8,128)(2,1)S(1)}, bf16[128,128]{1,0:T(8,128)(2,1)}, u32[]{:S(2)}) copy-start(bf16[128,128]{1,0:T(8,128)(2,1)} %w_key.1) | copy-start | bytes 98308
  26.7 5.9 %copy-start.3 = (bf16[128,128]{1,0:T(8,128)(2,1)S(1)}, bf16[128,128]{1,0:T(8,128)(2,1)}, u32[]{:S(2)}) copy-start(bf16[128,128]{1,0:T(8,128)(2,1)} %w_value.1) | copy-start | bytes 98308
  26.7 5.9 %copy-start.4 = (bf16[128,128]{1,0:T(8,128)(2,1)S(1)}, bf16[128,128]{1,0:T(8,128)(2,1)}, u32[]{:S(2)}) copy-start(bf16[128,128]{1,0:T(8,128)(2,1)} %w_msg.1) | copy-start | bytes 98308
  26.7 5.9 %copy-start.5 = (bf16[128,128]{1,0:T(8,128)(2,1)S(1)}, bf16[128,128]{1,0:T(8,128)(2,1)}, u32[]{:S(2)}) copy-start(bf16[128,128]{1,0:T(8,128)(2,1)} %w_out.1) | copy-start | bytes 98308
  26.7 16.4 %collective-permute-start.10 = (bf16[1024,128]{1,0:T(8,128)(2,1)S(1)}, bf16[1024,128]{1,0:T(8,128)(2,1)S(1)}, u32[]{:S(2)}, u32[]{:S(2)}) collective-permute-start(bf16[1024,128]{1,0:T(8,128)(2,1)S(1)} %shard_map.115), channel_id=1, source_target_pairs={{0,32},{32,0},{64,96},{96,64},{128,160},{160,128},{192,224},{224,1... | collective-permute-start | bytes 786440 | tf_op jit(solution)/shard_map/ppermute | solution.py:218
  27.3 15.9 %collective-permute-start.11 = (bf16[1024,128]{1,0:T(8,128)(2,1)S(1)}, bf16[1024,128]{1,0:T(8,128)(2,1)S(1)}, u32[]{:S(2)}, u32[]{:S(2)}) collective-permute-start(bf16[1024,128]{1,0:T(8,128)(2,1)S(1)} %shard_map.116), channel_id=1, source_target_pairs={{0,1},{1,0},{2,3},{3,2},{4,5},{5,4},{6,7},{7,6},{8,9},{9,8},{10,11... | collective-permute-start | bytes 786440 | tf_op jit(solution)/shard_map/ppermute | solution.py:218
  28.1 9.7 %collective-permute-start.1 = (bf16[512,128]{1,0:T(8,128)(2,1)S(1)}, bf16[512,128]{1,0:T(8,128)(2,1)S(1)}, u32[]{:S(2)}, u32[]{:S(2)}) collective-permute-start(bf16[512,128]{1,0:T(8,128)(2,1)S(1)} %get-tuple-element.26.border), channel_id=1, source_target_pairs={{0,224},{32,64},{64,32},{96,128},{128,96},{160,192},{192,160},{224... | collective-permute-start | bytes 393224 | tf_op jit(solution)/shard_map/ppermute | solution.py:218
  28.7 9.1 %collective-permute-start.4 = (bf16[512,128]{1,0:T(8,128)(2,1)S(1)}, bf16[512,128]{1,0:T(8,128)(2,1)S(1)}, u32[]{:S(2)}, u32[]{:S(2)}) collective-permute-start(bf16[512,128]{1,0:T(8,128)(2,1)S(1)} %get-tuple-element.26.border), channel_id=1, source_target_pairs={{0,1},{1,0},{2,3},{3,2},{4,5},{5,4},{6,7},{7,6},{8,9},{9,8},{10,11... | collective-permute-start | bytes 393224 | tf_op jit(solution)/shard_map/ppermute | solution.py:218
  29.5 8.4 %collective-permute-start.5 = (bf16[512,128]{1,0:T(8,128)(2,1)S(1)}, bf16[512,128]{1,0:T(8,128)(2,1)S(1)}, u32[]{:S(2)}, u32[]{:S(2)}) collective-permute-start(bf16[512,128]{1,0:T(8,128)(2,1)S(1)} %get-tuple-element.26.border), channel_id=1, source_target_pairs={{0,7},{1,2},{2,1},{3,4},{4,3},{5,6},{6,5},{7,0},{8,15},{9,10},{10,... | collective-permute-start | bytes 393224 | tf_op jit(solution)/shard_map/ppermute | solution.py:218
  34.1 3.8 %copy-start.6 = (s32[32,128]{1,0:T(8,128)S(1)}, s32[32,128]{1,0:T(8,128)}, u32[]{:S(2)}) copy-start(s32[32,128]{1,0:T(8,128)} %param.13) | copy-start | bytes 49156

commit v2 on v1

--- a/solution.py
+++ b/solution.py
@@ -13,7 +13,6 @@
 BF16 = jnp.bfloat16
 TILE = 128
 ROWS = 256
-NODES_STEP = 64
 VMEM_BYTES = 20 * 2**20
 
 VMEM = pl.BlockSpec(memory_space=pltpu.VMEM)
@@ -136,44 +135,45 @@
         top[here, :], acc[here, :] = absorb(q, keys[...], values[...], None, None)
 
 
-def edge_kernel(senders, own, xa, xb, ya, yb, za, zb, weights, recv, base, out, table, rows):
-    count, _ = own.shape
+def work_kernel(
+    senders, own, xa, xb, za, zb, weights, recv, base, top0, acc0, y0, y1, x0, x1, z0, z1,
+    node_part, line_y, top_x, acc_x, top_z, acc_z, table, rows, keys, values,
+):
+    count, width = own.shape
+    n = x0.shape[0]
     w_send = weight(weights, W_SEND)
     table[0:count, :] = dot(own[...], w_send)
-    for at, axis, pair in ((0, "gx", (xa, xb)), (2, "gy", (ya, yb)), (4, "gz", (za, zb))):
+    for at, axis, pair in ((0, "gx", (xa, xb)), (2, "gy", (y0, y1)), (4, "gz", (za, zb))):
         odd = lax.axis_index(axis) % 2
         low = pl.multiple_of(count + BND * (at + 1 - odd), BND)
         high = pl.multiple_of(count + BND * (at + odd), BND)
         table[pl.ds(low, BND), :] = dot(pair[0][:BND, :], w_send)
         table[pl.ds(high, BND), :] = dot(pair[1][:BND, :], w_send)
     w_sum = jnp.concatenate([weight(weights, W_MSG)] * 4, axis=0)
-
-    def gather(g, _):
-        for j in range(NODES_STEP):
+    project((y0.at[BND:, :], y1.at[BND:, :], x0, x1, z0, z1), weights, keys, values)
+
+    def gather(first, nodes):
+        for node in range(first, first + nodes):
             for d in range(4):
-                index = senders[g * NODES_STEP * 4 + j * 4 + d]
-                at = pl.multiple_of(g * NODES_STEP, NODES_STEP) + j
-                rows[d, pl.ds(at, 1), :] = table[pl.ds(index, 1), :]
-        return 0
-
-    lax.fori_loop(0, count // NODES_STEP, gather, 0)
-    hidden = jnp.concatenate([silu(rows[d] + recv[...]).astype(BF16) for d in range(4)], axis=1)
-    agg = dot(hidden, w_sum).astype(BF16)
-    out[...] = base[...] + dot(agg, weight(weights, W_AGG))
-
-
-def middle_kernel(own, weights, top0, acc0, y0, y1, x0, x1, z0, z1, line_y, top_x, acc_x, top_z, acc_z, keys, values):
-    count, width = own.shape
-    n = x0.shape[0]
-    project((y0.at[BND:, :], y1.at[BND:, :], x0, x1, z0, z1), weights, keys, values)
+                rows[d, node : node + 1, :] = table[pl.ds(senders[4 * node + d], 1), :]
+
+    def line(here, at):
+        return absorb(
+            own[here, :], keys[:, at : at + 3 * n], values[at : at + 3 * n, :], top0[here, :], acc0[here, :]
+        )
 
     for here in row_tiles(count, ROWS):
-        q = own[here, :]
-        t0, a0 = top0[here, :], acc0[here, :]
-        _, a = absorb(q, keys[:, 0 : 3 * n], values[0 : 3 * n, :], t0, a0)
+        gather(here.start, ROWS // 2)
+        _, a = line(here, 0)
         line_y[here, :] = a[:, :width] / a[:, width:]
-        top_x[here, :], acc_x[here, :] = absorb(q, keys[:, 3 * n : 6 * n], values[3 * n : 6 * n, :], t0, a0)
-        top_z[here, :], acc_z[here, :] = absorb(q, keys[:, 6 * n : 9 * n], values[6 * n : 9 * n, :], t0, a0)
+        gather(here.start + ROWS // 2, ROWS // 2)
+        top_x[here, :], acc_x[here, :] = line(here, 3 * n)
+        top_z[here, :], acc_z[here, :] = line(here, 6 * n)
+        hidden = jnp.concatenate(
+            [silu(rows[d, here, :] + recv[here, :]).astype(BF16) for d in range(4)], axis=1
+        )
+        agg = dot(hidden, w_sum).astype(BF16)
+        node_part[here, :] = base[here, :] + dot(agg, weight(weights, W_AGG))
 
 
 def final_kernel(
@@ -308,18 +308,17 @@
     z2 = exchange(stack((clusters, z0, z1)), "gz", lambda i: i ^ 1)
     x2 = exchange(stack((clusters, x0, x1)), "gx", lambda i: i ^ 1)
 
-    base = call(
-        edge_kernel,
-        (own, xa, xb, y0, y1, za, zb, weights, recv, base),
-        ((count, width), F32),
-        [((count + 6 * BND, width), F32), ((4, count, width), F32)],
+    base, line_y, top_x, acc_x, top_z, acc_z = call(
+        work_kernel,
+        (own, xa, xb, za, zb, weights, recv, base, top, acc, y0, y1, x0, x1, z0, z1),
+        [((count, width), F32)] * 2 + [((count, width), F32), ((count, 2 * width), F32)] * 2,
+        [
+            ((count + 6 * BND, width), F32),
+            ((4, count, width), F32),
+            ((width, 9 * n), BF16),
+            ((9 * n, 2 * width), BF16),
+        ],
         (senders.reshape(-1),),
-    )
-    line_y, top_x, acc_x, top_z, acc_z = call(
-        middle_kernel,
-        (own, weights, top, acc, y0, y1, x0, x1, z0, z1),
-        [((count, width), F32)] + [((count, width), F32), ((count, 2 * width), F32)] * 2,
-        [((width, 9 * n), BF16), ((9 * n, 2 * width), BF16)],
     )
     return call(
         final_kernel,

time: 47.7 us -> 46.8 us (0.981)
  the two profiles are of different devices: /device:TPU:1 before, /device:TPU:2 now
where the time goes in v2:
time: 46.8 us; the launch traced here: 46.7 us
  starting transfers between devices  25 us (53%)
  Pallas kernels  14.1 us (30%)
  waiting for transfers between devices  7.34 us (16%)
    ppermute x12, starting transfers between devices, exchange(): return lax.ppermute(x, axis, [(i, partner(i) % size) for i in range(size)])  25 us
    pallas_call x8, Pallas kernels, call(): pl.pallas_call(kernel, out_shape=[space(*o) for o in outs] if many else s...  12.9 us
    ppermute x12, waiting for transfers between devices, exchange(): return lax.ppermute(x, axis, [(i, partner(i) % size) for i in range(size)])  7.34 us
    pallas_call x1, Pallas kernels, on_device(): pl.pallas_call(load_kernel, out_shape=[pltpu.VMEM((count, width), BF16),...  1.26 us
  transfers between devices with their start and end apart: 12, of which 4 were waited for; matrix products, arithmetic and copies ran while one was open for 0% of the time, Pallas kernels for 18%

profile of v2, /device:TPU:2, one launch (start us, length us, event | category | flops | bytes accessed | tf_op | source)
XLA Modules:
  0.0 46.7 jit_solution(16688143346088543573)
XLA Ops:
  0.0 0.0 copy-start.7
  0.0 1.3 %load.1 = (bf16[1024,128]{1,0:T(8,128)(2,1)S(1)}, bf16[256,128]{1,0:T(8,128)(2,1)S(1)}, bf16[512,128]{1,0:T(8,128)(2,1)S(1)}, bf16[768,128]{1,0:T(8,128)(2,1)S(1...) custom-call(bf16[1024,128]{1,0:T(8,128)(2,1)} %own_far.1, bf16[256,128]{1,0:T(8,128)(2,1)} %clusters_far.1, ...), custom_call_target="tpu_custom_call" | custom-call | tf_op jit(solution)/shard_map/load/pallas_call | solution.py:246
  1.3 0.1 collective-permute-start.4
  1.4 0.0 copy-done.7
  1.4 3.3 %collective-permute-start.6 = (bf16[256,128]{1,0:T(8,128)(2,1)S(1)}, bf16[256,128]{1,0:T(8,128)(2,1)S(1)}, u32[]{:S(2)}, u32[]{:S(2)}) collective-permute-start(bf16[256,128]{1,0:T(8,128)(2,1)S(1)} %copy-done.7), channel_id=1, source_target_pairs={{0,64},{32,96},{64,0},{96,32},{128,192},{160,224},{192,128},{224,1... | collective-permute-start | bytes 196616 | tf_op jit(solution)/shard_map/ppermute | solution.py:218
  4.7 7.2 %collective-permute-start.8 = (bf16[256,128]{1,0:T(8,128)(2,1)S(1)}, bf16[256,128]{1,0:T(8,128)(2,1)S(1)}, u32[]{:S(2)}, u32[]{:S(2)}) collective-permute-start(bf16[256,128]{1,0:T(8,128)(2,1)S(1)} %copy-done.7), channel_id=1, source_target_pairs={{0,4},{1,5},{2,6},{3,7},{4,0},{5,1},{6,2},{7,3},{8,12},{9,13},{10,... | collective-permute-start | bytes 196616 | tf_op jit(solution)/shard_map/ppermute | solution.py:218
  11.9 0.0 collective-permute-done.6.refs_1_.x0
  11.9 2.2 %collective-permute-start.7 = (bf16[512,128]{1,0:T(8,128)(2,1)S(1)}, bf16[512,128]{1,0:T(8,128)(2,1)S(1)}, u32[]{:S(2)}, u32[]{:S(2)}) collective-permute-start(bf16[512,128]{1,0:T(8,128)(2,1)S(1)} %shard_map.111), channel_id=1, source_target_pairs={{0,128},{32,160},{64,192},{96,224},{128,0},{160,32},{192,64},{224,... | collective-permute-start | bytes 393224 | tf_op jit(solution)/shard_map/ppermute | solution.py:218
  14.1 0.3 collective-permute-done.8.refs_1_.z0
  14.4 3.2 %collective-permute-start.9 = (bf16[512,128]{1,0:T(8,128)(2,1)S(1)}, bf16[512,128]{1,0:T(8,128)(2,1)S(1)}, u32[]{:S(2)}, u32[]{:S(2)}) collective-permute-start(bf16[512,128]{1,0:T(8,128)(2,1)S(1)} %shard_map.112), channel_id=1, source_target_pairs={{0,2},{1,3},{2,0},{3,1},{4,6},{5,7},{6,4},{7,5},{8,10},{9,11},{10,... | collective-permute-start | bytes 393224 | tf_op jit(solution)/shard_map/ppermute | solution.py:218
  17.6 0.7 %collective-permute-start = (bf16[512,128]{1,0:T(8,128)(2,1)S(1)}, bf16[512,128]{1,0:T(8,128)(2,1)S(1)}, u32[]{:S(2)}, u32[]{:S(2)}) collective-permute-start(bf16[512,128]{1,0:T(8,128)(2,1)S(1)} %get-tuple-element.27.border), channel_id=1, source_target_pairs={{0,32},{32,0},{64,96},{96,64},{128,160},{160,128},{192,224},{224,1... | collective-permute-start | bytes 393224 | tf_op jit(solution)/shard_map/ppermute | solution.py:218
  18.2 1.9 %collective-permute-start.1 = (bf16[512,128]{1,0:T(8,128)(2,1)S(1)}, bf16[512,128]{1,0:T(8,128)(2,1)S(1)}, u32[]{:S(2)}, u32[]{:S(2)}) collective-permute-start(bf16[512,128]{1,0:T(8,128)(2,1)S(1)} %get-tuple-element.27.border), channel_id=1, source_target_pairs={{0,224},{32,64},{64,32},{96,128},{128,96},{160,192},{192,160},{224... | collective-permute-start | bytes 393224 | tf_op jit(solution)/shard_map/ppermute | solution.py:218
  20.2 0.0 collective-permute-done.4.came.y0
  20.2 0.1 collective-permute-start.5
  20.3 0.0 collective-permute-done.7.x1.refs_2_
  20.4 0.0 copy-start
  20.4 0.0 copy-start.1
  20.4 0.0 copy-start.2
  20.4 0.0 copy-start.3
  20.4 0.0 copy-start.4
  20.4 0.0 copy-start.5
  20.4 0.1 collective-permute-start.10
  20.5 2.5 %collective-permute-done.9.z1.refs_2_ = bf16[512,128]{1,0:T(8,128)(2,1)S(1)} collective-permute-done((bf16[512,128]{1,0:T(8,128)(2,1)S(1)}, bf16[512,128]{1,0:T(8,128)(2,1)S(1)}, u32[]{:S(2)}, u32[]{:S(2)}) %collective-permute-start.9) | collective-permute-done | bytes 131104 | tf_op jit(solution)/shard_map/ppermute | solution.py:218
  23.0 0.1 collective-permute-start.11
  23.1 0.0 collective-permute-done.xa
  23.1 2.0 %collective-permute-start.2 = (bf16[512,128]{1,0:T(8,128)(2,1)S(1)}, bf16[512,128]{1,0:T(8,128)(2,1)S(1)}, u32[]{:S(2)}, u32[]{:S(2)}) collective-permute-start(bf16[512,128]{1,0:T(8,128)(2,1)S(1)} %get-tuple-element.27.border), channel_id=1, source_target_pairs={{0,1},{1,0},{2,3},{3,2},{4,5},{5,4},{6,7},{7,6},{8,9},{9,8},{10,11... | collective-permute-start | bytes 393224 | tf_op jit(solution)/shard_map/ppermute | solution.py:218
  25.1 3.1 %collective-permute-done.1.xb = bf16[512,128]{1,0:T(8,128)(2,1)S(1)} collective-permute-done((bf16[512,128]{1,0:T(8,128)(2,1)S(1)}, bf16[512,128]{1,0:T(8,128)(2,1)S(1)}, u32[]{:S(2)}, u32[]{:S(2)}) %collective-permute-start.1) | collective-permute-done | bytes 131104 | tf_op jit(solution)/shard_map/ppermute | solution.py:218
  28.2 4.1 %collective-permute-start.3 = (bf16[512,128]{1,0:T(8,128)(2,1)S(1)}, bf16[512,128]{1,0:T(8,128)(2,1)S(1)}, u32[]{:S(2)}, u32[]{:S(2)}) collective-permute-start(bf16[512,128]{1,0:T(8,128)(2,1)S(1)} %get-tuple-element.27.border), channel_id=1, source_target_pairs={{0,7},{1,2},{2,1},{3,4},{4,3},{5,6},{6,5},{7,0},{8,15},{9,10},{10,... | collective-permute-start | bytes 393224 | tf_op jit(solution)/shard_map/ppermute | solution.py:218
  32.3 0.0 copy-done
  32.3 0.0 copy-done.1
  32.3 0.0 copy-done.2
  32.3 0.0 copy-done.3
  32.3 0.0 copy-done.4
  32.3 0.0 copy-done.5
  32.3 0.0 copy-start.6
  32.4 1.4 %shard_map.109 = (bf16[1280,128]{1,0:T(8,128)(2,1)S(1)}, f32[1024,128]{1,0:T(8,128)S(1)}, f32[1024,128]{1,0:T(8,128)S(1)}, f32[1024,128]{1,0:T(8,128)S(1)}, f32[1024,256]{1,0:T(8,128)S(1)}) custom-call(bf16[1024,128]{1,0:T(8,128)(2,1)S(1)} %get-tuple-element.22.own, bf16[256,128]{1,0:T(8,128)(2,1)S(1)} %get-tuple-element.23.clusters.refs_0_, ...), custom_call_target="tpu_custom_call" | custom-call | tf_op jit(solution)/shard_map/pallas_call | solution.py:206
  33.8 0.0 collective-permute-done.2.za
  33.8 1.5 %collective-permute-done.3.zb = bf16[512,128]{1,0:T(8,128)(2,1)S(1)} collective-permute-done((bf16[512,128]{1,0:T(8,128)(2,1)S(1)}, bf16[512,128]{1,0:T(8,128)(2,1)S(1)}, u32[]{:S(2)}, u32[]{:S(2)}) %collective-permute-start.3) | collective-permute-done | bytes 131104 | tf_op jit(solution)/shard_map/ppermute | solution.py:218
  35.3 0.0 collective-permute-done.5.y1
  35.3 0.0 copy-done.6
  35.3 7.0 %shard_map.113 = (f32[1024,128]{1,0:T(8,128)S(1)}, f32[1024,128]{1,0:T(8,128)S(1)}, f32[1024,128]{1,0:T(8,128)S(1)}, f32[1024,256]{1,0:T(8,128)S(1)}, f32[1024,128]{1,0:T(8,128)S(1)}, /*index=5*/f32[1024,256]{1,0:T(8,128)S(1)}) custom-call(s32[4096]{0:T(1024)S(1)} %bitcast.3, bf16[1024,128]{1,0:T(8,128)(2,1)S(1)} %get-tuple-element.22.own, ...), custom_call_target="tpu_custom_call" | custom-call | tf_op jit(solution)/shard_map/pallas_call | solution.py:206
  42.2 0.0 collective-permute-done.10.x2
  42.2 0.0 collective-permute-done.11.z2
  42.2 4.4 %shard_map.116 = bf16[1024,128]{1,0:T(8,128)(2,1)} custom-call(bf16[1024,128]{1,0:T(8,128)(2,1)S(1)} %get-tuple-element.22.own, bf16[1280,128]{1,0:T(8,128)(2,1)S(1)} %get-tuple-element.25.weights, f32[1,128]{1,0:T(1,128)S(1)} %get-tuple-element.26.gain, f32[1024,128]{1,0:T(8,128)S(1)} %get-tuple-element.33.base, f32[1024,128]{1,0:T(8,128)S(1)} %get-tuple-element.34.line_y, ...), custom_call_target="tpu_custom_call" | custom-call | tf_op jit(solution)/shard_map/pallas_call | solution.py:206
  (5 shorter events, 0.1 us)
Async XLA Ops:
  0.0 1.4 %copy-start.7 = (bf16[256,128]{1,0:T(8,128)(2,1)S(1)}, bf16[256,128]{1,0:T(8,128)(2,1)}, u32[]{:S(2)}) copy-start(bf16[256,128]{1,0:T(8,128)(2,1)} %clusters_far.1) | copy-start | bytes 196612
  1.3 18.9 %collective-permute-start.4 = (bf16[768,128]{1,0:T(8,128)(2,1)S(1)}, bf16[768,128]{1,0:T(8,128)(2,1)S(1)}, u32[]{:S(2)}, u32[]{:S(2)}) collective-permute-start(bf16[768,128]{1,0:T(8,128)(2,1)S(1)} %get-tuple-element.32), channel_id=1, source_target_pairs={{0,8},{8,0},{16,24},{24,16},{1,9},{9,1},{17,25},{25,17},{2,10},{10... | collective-permute-start | bytes 589832 | tf_op jit(solution)/shard_map/ppermute | solution.py:218
  1.4 10.5 %collective-permute-start.6 = (bf16[256,128]{1,0:T(8,128)(2,1)S(1)}, bf16[256,128]{1,0:T(8,128)(2,1)S(1)}, u32[]{:S(2)}, u32[]{:S(2)}) collective-permute-start(bf16[256,128]{1,0:T(8,128)(2,1)S(1)} %copy-done.7), channel_id=1, source_target_pairs={{0,64},{32,96},{64,0},{96,32},{128,192},{160,224},{192,128},{224,1... | collective-permute-start | bytes 196616 | tf_op jit(solution)/shard_map/ppermute | solution.py:218
  4.7 9.7 %collective-permute-start.8 = (bf16[256,128]{1,0:T(8,128)(2,1)S(1)}, bf16[256,128]{1,0:T(8,128)(2,1)S(1)}, u32[]{:S(2)}, u32[]{:S(2)}) collective-permute-start(bf16[256,128]{1,0:T(8,128)(2,1)S(1)} %copy-done.7), channel_id=1, source_target_pairs={{0,4},{1,5},{2,6},{3,7},{4,0},{5,1},{6,2},{7,3},{8,12},{9,13},{10,... | collective-permute-start | bytes 196616 | tf_op jit(solution)/shard_map/ppermute | solution.py:218
  11.9 8.4 %collective-permute-start.7 = (bf16[512,128]{1,0:T(8,128)(2,1)S(1)}, bf16[512,128]{1,0:T(8,128)(2,1)S(1)}, u32[]{:S(2)}, u32[]{:S(2)}) collective-permute-start(bf16[512,128]{1,0:T(8,128)(2,1)S(1)} %shard_map.111), channel_id=1, source_target_pairs={{0,128},{32,160},{64,192},{96,224},{128,0},{160,32},{192,64},{224,... | collective-permute-start | bytes 393224 | tf_op jit(solution)/shard_map/ppermute | solution.py:218
  14.4 8.6 %collective-permute-start.9 = (bf16[512,128]{1,0:T(8,128)(2,1)S(1)}, bf16[512,128]{1,0:T(8,128)(2,1)S(1)}, u32[]{:S(2)}, u32[]{:S(2)}) collective-permute-start(bf16[512,128]{1,0:T(8,128)(2,1)S(1)} %shard_map.112), channel_id=1, source_target_pairs={{0,2},{1,3},{2,0},{3,1},{4,6},{5,7},{6,4},{7,5},{8,10},{9,11},{10,... | collective-permute-start | bytes 393224 | tf_op jit(solution)/shard_map/ppermute | solution.py:218
  17.6 5.5 %collective-permute-start = (bf16[512,128]{1,0:T(8,128)(2,1)S(1)}, bf16[512,128]{1,0:T(8,128)(2,1)S(1)}, u32[]{:S(2)}, u32[]{:S(2)}) collective-permute-start(bf16[512,128]{1,0:T(8,128)(2,1)S(1)} %get-tuple-element.27.border), channel_id=1, source_target_pairs={{0,32},{32,0},{64,96},{96,64},{128,160},{160,128},{192,224},{224,1... | collective-permute-start | bytes 393224 | tf_op jit(solution)/shard_map/ppermute | solution.py:218
  18.2 10.0 %collective-permute-start.1 = (bf16[512,128]{1,0:T(8,128)(2,1)S(1)}, bf16[512,128]{1,0:T(8,128)(2,1)S(1)}, u32[]{:S(2)}, u32[]{:S(2)}) collective-permute-start(bf16[512,128]{1,0:T(8,128)(2,1)S(1)} %get-tuple-element.27.border), channel_id=1, source_target_pairs={{0,224},{32,64},{64,32},{96,128},{128,96},{160,192},{192,160},{224... | collective-permute-start | bytes 393224 | tf_op jit(solution)/shard_map/ppermute | solution.py:218
  20.2 15.0 %collective-permute-start.5 = (bf16[1024,128]{1,0:T(8,128)(2,1)S(1)}, bf16[1024,128]{1,0:T(8,128)(2,1)S(1)}, u32[]{:S(2)}, u32[]{:S(2)}) collective-permute-start(bf16[1024,128]{1,0:T(8,128)(2,1)S(1)} %shard_map.110), channel_id=1, source_target_pairs={{0,24},{8,16},{16,8},{24,0},{1,25},{9,17},{17,9},{25,1},{2,26},{10... | collective-permute-start | bytes 786440 | tf_op jit(solution)/shard_map/ppermute | solution.py:218
  20.4 12.0 %copy-start = (bf16[512,128]{1,0:T(8,128)(2,1)S(1)}, bf16[512,128]{1,0:T(8,128)(2,1)}, u32[]{:S(2)}) copy-start(bf16[512,128]{1,0:T(8,128)(2,1)} %w_node.1) | copy-start | bytes 393220
  20.4 12.0 %copy-start.1 = (bf16[256,128]{1,0:T(8,128)(2,1)S(1)}, bf16[256,128]{1,0:T(8,128)(2,1)}, u32[]{:S(2)}) copy-start(bf16[256,128]{1,0:T(8,128)(2,1)} %w_in.1) | copy-start | bytes 196612
  20.4 11.9 %copy-start.2 = (bf16[128,128]{1,0:T(8,128)(2,1)S(1)}, bf16[128,128]{1,0:T(8,128)(2,1)}, u32[]{:S(2)}) copy-start(bf16[128,128]{1,0:T(8,128)(2,1)} %w_key.1) | copy-start | bytes 98308
  20.4 11.9 %copy-start.3 = (bf16[128,128]{1,0:T(8,128)(2,1)S(1)}, bf16[128,128]{1,0:T(8,128)(2,1)}, u32[]{:S(2)}) copy-start(bf16[128,128]{1,0:T(8,128)(2,1)} %w_value.1) | copy-start | bytes 98308
  20.4 11.9 %copy-start.4 = (bf16[128,128]{1,0:T(8,128)(2,1)S(1)}, bf16[128,128]{1,0:T(8,128)(2,1)}, u32[]{:S(2)}) copy-start(bf16[128,128]{1,0:T(8,128)(2,1)} %w_msg.1) | copy-start | bytes 98308
  20.4 11.9 %copy-start.5 = (bf16[128,128]{1,0:T(8,128)(2,1)S(1)}, bf16[128,128]{1,0:T(8,128)(2,1)}, u32[]{:S(2)}) copy-start(bf16[128,128]{1,0:T(8,128)(2,1)} %w_out.1) | copy-start | bytes 98308
  20.4 21.8 %collective-permute-start.10 = (bf16[1024,128]{1,0:T(8,128)(2,1)S(1)}, bf16[1024,128]{1,0:T(8,128)(2,1)S(1)}, u32[]{:S(2)}, u32[]{:S(2)}) collective-permute-start(bf16[1024,128]{1,0:T(8,128)(2,1)S(1)} %shard_map.114), channel_id=1, source_target_pairs={{0,32},{32,0},{64,96},{96,64},{128,160},{160,128},{192,224},{224,1... | collective-permute-start | bytes 786440 | tf_op jit(solution)/shard_map/ppermute | solution.py:218
  23.0 19.2 %collective-permute-start.11 = (bf16[1024,128]{1,0:T(8,128)(2,1)S(1)}, bf16[1024,128]{1,0:T(8,128)(2,1)S(1)}, u32[]{:S(2)}, u32[]{:S(2)}) collective-permute-start(bf16[1024,128]{1,0:T(8,128)(2,1)S(1)} %shard_map.115), channel_id=1, source_target_pairs={{0,1},{1,0},{2,3},{3,2},{4,5},{5,4},{6,7},{7,6},{8,9},{9,8},{10,11... | collective-permute-start | bytes 786440 | tf_op jit(solution)/shard_map/ppermute | solution.py:218
  23.1 10.6 %collective-permute-start.2 = (bf16[512,128]{1,0:T(8,128)(2,1)S(1)}, bf16[512,128]{1,0:T(8,128)(2,1)S(1)}, u32[]{:S(2)}, u32[]{:S(2)}) collective-permute-start(bf16[512,128]{1,0:T(8,128)(2,1)S(1)} %get-tuple-element.27.border), channel_id=1, source_target_pairs={{0,1},{1,0},{2,3},{3,2},{4,5},{5,4},{6,7},{7,6},{8,9},{9,8},{10,11... | collective-permute-start | bytes 393224 | tf_op jit(solution)/shard_map/ppermute | solution.py:218
  28.2 7.0 %collective-permute-start.3 = (bf16[512,128]{1,0:T(8,128)(2,1)S(1)}, bf16[512,128]{1,0:T(8,128)(2,1)S(1)}, u32[]{:S(2)}, u32[]{:S(2)}) collective-permute-start(bf16[512,128]{1,0:T(8,128)(2,1)S(1)} %get-tuple-element.27.border), channel_id=1, source_target_pairs={{0,7},{1,2},{2,1},{3,4},{4,3},{5,6},{6,5},{7,0},{8,15},{9,10},{10,... | collective-permute-start | bytes 393224 | tf_op jit(solution)/shard_map/ppermute | solution.py:218
  32.3 2.9 %copy-start.6 = (s32[32,128]{1,0:T(8,128)S(1)}, s32[32,128]{1,0:T(8,128)}, u32[]{:S(2)}) copy-start(s32[32,128]{1,0:T(8,128)} %param.13) | copy-start | bytes 49156

commit v3 on v2

--- a/solution.py
+++ b/solution.py
@@ -135,11 +135,19 @@
         top[here, :], acc[here, :] = absorb(q, keys[...], values[...], None, None)
 
 
+def line_y_kernel(own, weights, top0, acc0, y0, y1, line_y, keys, values):
+    count, width = own.shape
+    project((y0.at[BND:, :], y1.at[BND:, :]), weights, keys, values)
+    for here in row_tiles(count, ROWS):
+        _, a = absorb(own[here, :], keys[...], values[...], top0[here, :], acc0[here, :])
+        line_y[here, :] = a[:, :width] / a[:, width:]
+
+
 def work_kernel(
     senders, own, xa, xb, za, zb, weights, recv, base, top0, acc0, y0, y1, x0, x1, z0, z1,
-    node_part, line_y, top_x, acc_x, top_z, acc_z, table, rows, keys, values,
-):
-    count, width = own.shape
+    node_part, top_x, acc_x, top_z, acc_z, table, rows, keys, values,
+):
+    count, _ = own.shape
     n = x0.shape[0]
     w_send = weight(weights, W_SEND)
     table[0:count, :] = dot(own[...], w_send)
@@ -150,7 +158,7 @@
         table[pl.ds(low, BND), :] = dot(pair[0][:BND, :], w_send)
         table[pl.ds(high, BND), :] = dot(pair[1][:BND, :], w_send)
     w_sum = jnp.concatenate([weight(weights, W_MSG)] * 4, axis=0)
-    project((y0.at[BND:, :], y1.at[BND:, :], x0, x1, z0, z1), weights, keys, values)
+    project((x0, x1, z0, z1), weights, keys, values)
 
     def gather(first, nodes):
         for node in range(first, first + nodes):
@@ -164,11 +172,9 @@
 
     for here in row_tiles(count, ROWS):
         gather(here.start, ROWS // 2)
-        _, a = line(here, 0)
-        line_y[here, :] = a[:, :width] / a[:, width:]
+        top_x[here, :], acc_x[here, :] = line(here, 0)
         gather(here.start + ROWS // 2, ROWS // 2)
-        top_x[here, :], acc_x[here, :] = line(here, 3 * n)
-        top_z[here, :], acc_z[here, :] = line(here, 6 * n)
+        top_z[here, :], acc_z[here, :] = line(here, 3 * n)
         hidden = jnp.concatenate(
             [silu(rows[d, here, :] + recv[here, :]).astype(BF16) for d in range(4)], axis=1
         )
@@ -242,7 +248,7 @@
         return call(stack_kernel, pieces, ((sum(p.shape[0] for p in pieces), width), BF16))
 
     z0 = exchange(cluster_latents, "gz", lambda i: i ^ 4)
-    x0 = exchange(cluster_latents, "gx", lambda i: i ^ 2)
+    x0 = exchange(cluster_latents, "gx", lambda i: i ^ 4)
     own, clusters, border, both, member, gain = pl.pallas_call(
         load_kernel,
         out_shape=[
@@ -298,7 +304,7 @@
         [((width, n), BF16), ((n, 2 * width), BF16)],
     )
 
-    x1 = exchange(stack((clusters, x0)), "gx", lambda i: i ^ 4)
+    x1 = exchange(stack((clusters, x0)), "gx", lambda i: i ^ 2)
     y1 = exchange(
         call(stack_after_border_kernel, (border, clusters, y0), ((BND + 2 * n, width), BF16)),
         "gy",
@@ -308,15 +314,21 @@
     z2 = exchange(stack((clusters, z0, z1)), "gz", lambda i: i ^ 1)
     x2 = exchange(stack((clusters, x0, x1)), "gx", lambda i: i ^ 1)
 
-    base, line_y, top_x, acc_x, top_z, acc_z = call(
+    line_y = call(
+        line_y_kernel,
+        (own, weights, top, acc, y0, y1),
+        ((count, width), F32),
+        [((width, 3 * n), BF16), ((3 * n, 2 * width), BF16)],
+    )
+    base, top_x, acc_x, top_z, acc_z = call(
         work_kernel,
         (own, xa, xb, za, zb, weights, recv, base, top, acc, y0, y1, x0, x1, z0, z1),
-        [((count, width), F32)] * 2 + [((count, width), F32), ((count, 2 * width), F32)] * 2,
+        [((count, width), F32)] + [((count, width), F32), ((count, 2 * width), F32)] * 2,
         [
             ((count + 6 * BND, width), F32),
             ((4, count, width), F32),
-            ((width, 9 * n), BF16),
-            ((9 * n, 2 * width), BF16),
+            ((width, 6 * n), BF16),
+            ((6 * n, 2 * width), BF16),
         ],
         (senders.reshape(-1),),
     )

time: 46.8 us -> 45.8 us (0.979)
  waiting for transfers between devices: 7.34 us -> 4.63 us
  starting transfers between devices: 25 us -> 26.2 us
  Pallas kernels: 14.1 us -> 14.6 us
    ppermute x12, waiting for transfers between devices: 7.34 us -> 4.63 us  [exchange(): return lax.ppermute(x, axis, [(i, partner(i) % size) for i in range(size)])]
    ppermute x12, starting transfers between devices: 25 us -> 26.2 us  [exchange(): return lax.ppermute(x, axis, [(i, partner(i) % size) for i in range(size)])]
    pallas_call x8 -> x9, Pallas kernels: 12.9 us -> 13.4 us  [call(): pl.pallas_call(kernel, out_shape=[space(*o) for o in outs] if many else s...]
  transfers between devices with their start and end apart: 12 -> 12, of which waited for: 4 -> 3; matrix products, arithmetic and copies ran while one was open for 0% -> 0% of each run, Pallas kernels for 18% -> 20%
where the time goes in v3:
time: 45.8 us; the launch traced here: 45.7 us
  starting transfers between devices  26.2 us (57%)
  Pallas kernels  14.6 us (32%)
  waiting for transfers between devices  4.63 us (10%)
    ppermute x12, starting transfers between devices, exchange(): return lax.ppermute(x, axis, [(i, partner(i) % size) for i in range(size)])  26.2 us
    pallas_call x9, Pallas kernels, call(): pl.pallas_call(kernel, out_shape=[space(*o) for o in outs] if many else s...  13.4 us
    ppermute x12, waiting for transfers between devices, exchange(): return lax.ppermute(x, axis, [(i, partner(i) % size) for i in range(size)])  4.63 us
    pallas_call x1, Pallas kernels, on_device(): pl.pallas_call(load_kernel, out_shape=[pltpu.VMEM((count, width), BF16),...  1.26 us
  transfers between devices with their start and end apart: 12, of which 3 were waited for; matrix products, arithmetic and copies ran while one was open for 0% of the time, Pallas kernels for 20%

profile of v3, /device:TPU:2, one launch (start us, length us, event | category | flops | bytes accessed | tf_op | source)
XLA Modules:
  0.0 45.7 jit_solution(17141291618709873394)
XLA Ops:
  0.0 0.0 copy-start.7
  0.0 1.3 %load.1 = (bf16[1024,128]{1,0:T(8,128)(2,1)S(1)}, bf16[256,128]{1,0:T(8,128)(2,1)S(1)}, bf16[512,128]{1,0:T(8,128)(2,1)S(1)}, bf16[768,128]{1,0:T(8,128)(2,1)S(1...) custom-call(bf16[1024,128]{1,0:T(8,128)(2,1)} %own_far.1, bf16[256,128]{1,0:T(8,128)(2,1)} %clusters_far.1, ...), custom_call_target="tpu_custom_call" | custom-call | tf_op jit(solution)/shard_map/load/pallas_call | solution.py:252
  1.3 0.1 collective-permute-start.4
  1.4 0.0 copy-done.7
  1.4 2.2 %collective-permute-start.6 = (bf16[256,128]{1,0:T(8,128)(2,1)S(1)}, bf16[256,128]{1,0:T(8,128)(2,1)S(1)}, u32[]{:S(2)}, u32[]{:S(2)}) collective-permute-start(bf16[256,128]{1,0:T(8,128)(2,1)S(1)} %copy-done.7), channel_id=1, source_target_pairs={{0,128},{32,160},{64,192},{96,224},{128,0},{160,32},{192,64},{224,... | collective-permute-start | bytes 196616 | tf_op jit(solution)/shard_map/ppermute | solution.py:224
  3.6 7.2 %collective-permute-start.8 = (bf16[256,128]{1,0:T(8,128)(2,1)S(1)}, bf16[256,128]{1,0:T(8,128)(2,1)S(1)}, u32[]{:S(2)}, u32[]{:S(2)}) collective-permute-start(bf16[256,128]{1,0:T(8,128)(2,1)S(1)} %copy-done.7), channel_id=1, source_target_pairs={{0,4},{1,5},{2,6},{3,7},{4,0},{5,1},{6,2},{7,3},{8,12},{9,13},{10,... | collective-permute-start | bytes 196616 | tf_op jit(solution)/shard_map/ppermute | solution.py:224
  10.8 0.0 collective-permute-done.4.came.y0
  10.8 1.0 %collective-permute-start.5 = (bf16[1024,128]{1,0:T(8,128)(2,1)S(1)}, bf16[1024,128]{1,0:T(8,128)(2,1)S(1)}, u32[]{:S(2)}, u32[]{:S(2)}) collective-permute-start(bf16[1024,128]{1,0:T(8,128)(2,1)S(1)} %shard_map.110), channel_id=1, source_target_pairs={{0,24},{8,16},{16,8},{24,0},{1,25},{9,17},{17,9},{25,1},{2,26},{10... | collective-permute-start | bytes 786440 | tf_op jit(solution)/shard_map/ppermute | solution.py:224
  11.8 0.0 collective-permute-done.6.refs_1_.x0
  11.8 3.3 %collective-permute-start.7 = (bf16[512,128]{1,0:T(8,128)(2,1)S(1)}, bf16[512,128]{1,0:T(8,128)(2,1)S(1)}, u32[]{:S(2)}, u32[]{:S(2)}) collective-permute-start(bf16[512,128]{1,0:T(8,128)(2,1)S(1)} %shard_map.111), channel_id=1, source_target_pairs={{0,64},{32,96},{64,0},{96,32},{128,192},{160,224},{192,128},{224,1... | collective-permute-start | bytes 393224 | tf_op jit(solution)/shard_map/ppermute | solution.py:224
  15.1 0.0 collective-permute-done.8.refs_1_.z0
  15.1 1.6 %collective-permute-start.9 = (bf16[512,128]{1,0:T(8,128)(2,1)S(1)}, bf16[512,128]{1,0:T(8,128)(2,1)S(1)}, u32[]{:S(2)}, u32[]{:S(2)}) collective-permute-start(bf16[512,128]{1,0:T(8,128)(2,1)S(1)} %shard_map.112), channel_id=1, source_target_pairs={{0,2},{1,3},{2,0},{3,1},{4,6},{5,7},{6,4},{7,5},{8,10},{9,11},{10,... | collective-permute-start | bytes 393224 | tf_op jit(solution)/shard_map/ppermute | solution.py:224
  16.7 1.4 %collective-permute-start = (bf16[512,128]{1,0:T(8,128)(2,1)S(1)}, bf16[512,128]{1,0:T(8,128)(2,1)S(1)}, u32[]{:S(2)}, u32[]{:S(2)}) collective-permute-start(bf16[512,128]{1,0:T(8,128)(2,1)S(1)} %get-tuple-element.26.border), channel_id=1, source_target_pairs={{0,32},{32,0},{64,96},{96,64},{128,160},{160,128},{192,224},{224,1... | collective-permute-start | bytes 393224 | tf_op jit(solution)/shard_map/ppermute | solution.py:224
  18.1 1.4 %collective-permute-done.7.x1.refs_2_ = bf16[512,128]{1,0:T(8,128)(2,1)S(1)} collective-permute-done((bf16[512,128]{1,0:T(8,128)(2,1)S(1)}, bf16[512,128]{1,0:T(8,128)(2,1)S(1)}, u32[]{:S(2)}, u32[]{:S(2)}) %collective-permute-start.7) | collective-permute-done | bytes 131104 | tf_op jit(solution)/shard_map/ppermute | solution.py:224
  19.5 0.0 copy-start
  19.5 0.0 copy-start.1
  19.5 0.0 copy-start.2
  19.5 0.0 copy-start.3
  19.5 0.0 copy-start.4
  19.5 0.0 copy-start.5
  19.6 2.0 %collective-permute-start.10 = (bf16[1024,128]{1,0:T(8,128)(2,1)S(1)}, bf16[1024,128]{1,0:T(8,128)(2,1)S(1)}, u32[]{:S(2)}, u32[]{:S(2)}) collective-permute-start(bf16[1024,128]{1,0:T(8,128)(2,1)S(1)} %shard_map.115), channel_id=1, source_target_pairs={{0,32},{32,0},{64,96},{96,64},{128,160},{160,128},{192,224},{224,1... | collective-permute-start | bytes 786440 | tf_op jit(solution)/shard_map/ppermute | solution.py:224
  21.5 3.2 %collective-permute-done.9.z1.refs_2_ = bf16[512,128]{1,0:T(8,128)(2,1)S(1)} collective-permute-done((bf16[512,128]{1,0:T(8,128)(2,1)S(1)}, bf16[512,128]{1,0:T(8,128)(2,1)S(1)}, u32[]{:S(2)}, u32[]{:S(2)}) %collective-permute-start.9) | collective-permute-done | bytes 131104 | tf_op jit(solution)/shard_map/ppermute | solution.py:224
  24.7 0.1 collective-permute-start.11
  24.8 1.2 %collective-permute-start.1 = (bf16[512,128]{1,0:T(8,128)(2,1)S(1)}, bf16[512,128]{1,0:T(8,128)(2,1)S(1)}, u32[]{:S(2)}, u32[]{:S(2)}) collective-permute-start(bf16[512,128]{1,0:T(8,128)(2,1)S(1)} %get-tuple-element.26.border), channel_id=1, source_target_pairs={{0,224},{32,64},{64,32},{96,128},{128,96},{160,192},{192,160},{224... | collective-permute-start | bytes 393224 | tf_op jit(solution)/shard_map/ppermute | solution.py:224
  26.0 0.0 collective-permute-done.xa
  26.0 1.9 %collective-permute-start.2 = (bf16[512,128]{1,0:T(8,128)(2,1)S(1)}, bf16[512,128]{1,0:T(8,128)(2,1)S(1)}, u32[]{:S(2)}, u32[]{:S(2)}) collective-permute-start(bf16[512,128]{1,0:T(8,128)(2,1)S(1)} %get-tuple-element.26.border), channel_id=1, source_target_pairs={{0,1},{1,0},{2,3},{3,2},{4,5},{5,4},{6,7},{7,6},{8,9},{9,8},{10,11... | collective-permute-start | bytes 393224 | tf_op jit(solution)/shard_map/ppermute | solution.py:224
  27.9 0.0 collective-permute-done.5.y1
  27.9 4.3 %collective-permute-start.3 = (bf16[512,128]{1,0:T(8,128)(2,1)S(1)}, bf16[512,128]{1,0:T(8,128)(2,1)S(1)}, u32[]{:S(2)}, u32[]{:S(2)}) collective-permute-start(bf16[512,128]{1,0:T(8,128)(2,1)S(1)} %get-tuple-element.26.border), channel_id=1, source_target_pairs={{0,7},{1,2},{2,1},{3,4},{4,3},{5,6},{6,5},{7,0},{8,15},{9,10},{10,... | collective-permute-start | bytes 393224 | tf_op jit(solution)/shard_map/ppermute | solution.py:224
  32.3 0.0 copy-done
  32.3 0.0 copy-done.1
  32.3 0.0 copy-done.2
  32.3 0.0 copy-done.3
  32.3 0.0 copy-done.4
  32.3 0.0 copy-done.5
  32.3 1.4 %shard_map.109 = (bf16[1280,128]{1,0:T(8,128)(2,1)S(1)}, f32[1024,128]{1,0:T(8,128)S(1)}, f32[1024,128]{1,0:T(8,128)S(1)}, f32[1024,128]{1,0:T(8,128)S(1)}, f32[1024,256]{1,0:T(8,128)S(1)}) custom-call(bf16[1024,128]{1,0:T(8,128)(2,1)S(1)} %get-tuple-element.21.own, bf16[256,128]{1,0:T(8,128)(2,1)S(1)} %get-tuple-element.22.clusters.refs_0_, ...), custom_call_target="tpu_custom_call" | custom-call | tf_op jit(solution)/shard_map/pallas_call | solution.py:212
  33.7 0.0 copy-start.6
  33.7 1.6 %shard_map.114.line_y = f32[1024,128]{1,0:T(8,128)S(1)} custom-call(bf16[1024,128]{1,0:T(8,128)(2,1)S(1)} %get-tuple-element.21.own, bf16[1280,128]{1,0:T(8,128)(2,1)S(1)} %get-tuple-element.24.weights, f32[1024,128]{1,0:T(8,128)S(1)} %get-tuple-element.29.top0, f32[1024,256]{1,0:T(8,128)S(1)} %get-tuple-element.30.acc0, ...), custom_call_target="tpu_custom_call" | custom-call | tf_op jit(solution)/shard_map/pallas_call | solution.py:212
  35.3 0.0 collective-permute-done.1.xb
  35.3 0.1 collective-permute-done.2.za
  35.4 0.0 collective-permute-done.3.zb
  35.4 0.0 copy-done.6
  35.4 5.9 %shard_map.113 = (f32[1024,128]{1,0:T(8,128)S(1)}, f32[1024,128]{1,0:T(8,128)S(1)}, f32[1024,256]{1,0:T(8,128)S(1)}, f32[1024,128]{1,0:T(8,128)S(1)}, f32[1024,256]{1,0:T(8,128)S(1)}) custom-call(s32[4096]{0:T(1024)S(1)} %bitcast.3, bf16[1024,128]{1,0:T(8,128)(2,1)S(1)} %get-tuple-element.21.own, bf16[512,128]{1,0:T(8,128)(2,1)S(1)} %collective-permute-done.xa, ...), custom_call_target="tpu_custom_call" | custom-call | tf_op jit(solution)/shard_map/pallas_call | solution.py:212
  41.3 0.0 collective-permute-done.10.x2
  41.3 0.0 collective-permute-done.11.z2
  41.3 4.4 %shard_map.117 = bf16[1024,128]{1,0:T(8,128)(2,1)} custom-call(bf16[1024,128]{1,0:T(8,128)(2,1)S(1)} %get-tuple-element.21.own, bf16[1280,128]{1,0:T(8,128)(2,1)S(1)} %get-tuple-element.24.weights, f32[1,128]{1,0:T(1,128)S(1)} %get-tuple-element.25.gain, f32[1024,128]{1,0:T(8,128)S(1)} %get-tuple-element.32.base, f32[1024,128]{1,0:T(8,128)S(1)} %shard_map.114.line_y, ...), custom_call_target="tpu_custom_call" | custom-call | tf_op jit(solution)/shard_map/pallas_call | solution.py:212
  (5 shorter events, 0.1 us)
Async XLA Ops:
  0.0 1.4 %copy-start.7 = (bf16[256,128]{1,0:T(8,128)(2,1)S(1)}, bf16[256,128]{1,0:T(8,128)(2,1)}, u32[]{:S(2)}) copy-start(bf16[256,128]{1,0:T(8,128)(2,1)} %clusters_far.1) | copy-start | bytes 196612
  1.3 9.5 %collective-permute-start.4 = (bf16[768,128]{1,0:T(8,128)(2,1)S(1)}, bf16[768,128]{1,0:T(8,128)(2,1)S(1)}, u32[]{:S(2)}, u32[]{:S(2)}) collective-permute-start(bf16[768,128]{1,0:T(8,128)(2,1)S(1)} %get-tuple-element.31), channel_id=1, source_target_pairs={{0,8},{8,0},{16,24},{24,16},{1,9},{9,1},{17,25},{25,17},{2,10},{10... | collective-permute-start | bytes 589832 | tf_op jit(solution)/shard_map/ppermute | solution.py:224
  1.4 10.4 %collective-permute-start.6 = (bf16[256,128]{1,0:T(8,128)(2,1)S(1)}, bf16[256,128]{1,0:T(8,128)(2,1)S(1)}, u32[]{:S(2)}, u32[]{:S(2)}) collective-permute-start(bf16[256,128]{1,0:T(8,128)(2,1)S(1)} %copy-done.7), channel_id=1, source_target_pairs={{0,128},{32,160},{64,192},{96,224},{128,0},{160,32},{192,64},{224,... | collective-permute-start | bytes 196616 | tf_op jit(solution)/shard_map/ppermute | solution.py:224
  3.6 11.5 %collective-permute-start.8 = (bf16[256,128]{1,0:T(8,128)(2,1)S(1)}, bf16[256,128]{1,0:T(8,128)(2,1)S(1)}, u32[]{:S(2)}, u32[]{:S(2)}) collective-permute-start(bf16[256,128]{1,0:T(8,128)(2,1)S(1)} %copy-done.7), channel_id=1, source_target_pairs={{0,4},{1,5},{2,6},{3,7},{4,0},{5,1},{6,2},{7,3},{8,12},{9,13},{10,... | collective-permute-start | bytes 196616 | tf_op jit(solution)/shard_map/ppermute | solution.py:224
  10.8 17.1 %collective-permute-start.5 = (bf16[1024,128]{1,0:T(8,128)(2,1)S(1)}, bf16[1024,128]{1,0:T(8,128)(2,1)S(1)}, u32[]{:S(2)}, u32[]{:S(2)}) collective-permute-start(bf16[1024,128]{1,0:T(8,128)(2,1)S(1)} %shard_map.110), channel_id=1, source_target_pairs={{0,24},{8,16},{16,8},{24,0},{1,25},{9,17},{17,9},{25,1},{2,26},{10... | collective-permute-start | bytes 786440 | tf_op jit(solution)/shard_map/ppermute | solution.py:224
  11.8 7.7 %collective-permute-start.7 = (bf16[512,128]{1,0:T(8,128)(2,1)S(1)}, bf16[512,128]{1,0:T(8,128)(2,1)S(1)}, u32[]{:S(2)}, u32[]{:S(2)}) collective-permute-start(bf16[512,128]{1,0:T(8,128)(2,1)S(1)} %shard_map.111), channel_id=1, source_target_pairs={{0,64},{32,96},{64,0},{96,32},{128,192},{160,224},{192,128},{224,1... | collective-permute-start | bytes 393224 | tf_op jit(solution)/shard_map/ppermute | solution.py:224
  15.1 9.6 %collective-permute-start.9 = (bf16[512,128]{1,0:T(8,128)(2,1)S(1)}, bf16[512,128]{1,0:T(8,128)(2,1)S(1)}, u32[]{:S(2)}, u32[]{:S(2)}) collective-permute-start(bf16[512,128]{1,0:T(8,128)(2,1)S(1)} %shard_map.112), channel_id=1, source_target_pairs={{0,2},{1,3},{2,0},{3,1},{4,6},{5,7},{6,4},{7,5},{8,10},{9,11},{10,... | collective-permute-start | bytes 393224 | tf_op jit(solution)/shard_map/ppermute | solution.py:224
  16.7 9.3 %collective-permute-start = (bf16[512,128]{1,0:T(8,128)(2,1)S(1)}, bf16[512,128]{1,0:T(8,128)(2,1)S(1)}, u32[]{:S(2)}, u32[]{:S(2)}) collective-permute-start(bf16[512,128]{1,0:T(8,128)(2,1)S(1)} %get-tuple-element.26.border), channel_id=1, source_target_pairs={{0,32},{32,0},{64,96},{96,64},{128,160},{160,128},{192,224},{224,1... | collective-permute-start | bytes 393224 | tf_op jit(solution)/shard_map/ppermute | solution.py:224
  19.5 12.8 %copy-start = (bf16[512,128]{1,0:T(8,128)(2,1)S(1)}, bf16[512,128]{1,0:T(8,128)(2,1)}, u32[]{:S(2)}) copy-start(bf16[512,128]{1,0:T(8,128)(2,1)} %w_node.1) | copy-start | bytes 393220
  19.5 12.8 %copy-start.1 = (bf16[256,128]{1,0:T(8,128)(2,1)S(1)}, bf16[256,128]{1,0:T(8,128)(2,1)}, u32[]{:S(2)}) copy-start(bf16[256,128]{1,0:T(8,128)(2,1)} %w_in.1) | copy-start | bytes 196612
  19.5 12.8 %copy-start.2 = (bf16[128,128]{1,0:T(8,128)(2,1)S(1)}, bf16[128,128]{1,0:T(8,128)(2,1)}, u32[]{:S(2)}) copy-start(bf16[128,128]{1,0:T(8,128)(2,1)} %w_key.1) | copy-start | bytes 98308
  19.5 12.7 %copy-start.3 = (bf16[128,128]{1,0:T(8,128)(2,1)S(1)}, bf16[128,128]{1,0:T(8,128)(2,1)}, u32[]{:S(2)}) copy-start(bf16[128,128]{1,0:T(8,128)(2,1)} %w_value.1) | copy-start | bytes 98308
  19.5 12.7 %copy-start.4 = (bf16[128,128]{1,0:T(8,128)(2,1)S(1)}, bf16[128,128]{1,0:T(8,128)(2,1)}, u32[]{:S(2)}) copy-start(bf16[128,128]{1,0:T(8,128)(2,1)} %w_msg.1) | copy-start | bytes 98308
  19.5 12.7 %copy-start.5 = (bf16[128,128]{1,0:T(8,128)(2,1)S(1)}, bf16[128,128]{1,0:T(8,128)(2,1)}, u32[]{:S(2)}) copy-start(bf16[128,128]{1,0:T(8,128)(2,1)} %w_out.1) | copy-start | bytes 98308
  19.6 21.8 %collective-permute-start.10 = (bf16[1024,128]{1,0:T(8,128)(2,1)S(1)}, bf16[1024,128]{1,0:T(8,128)(2,1)S(1)}, u32[]{:S(2)}, u32[]{:S(2)}) collective-permute-start(bf16[1024,128]{1,0:T(8,128)(2,1)S(1)} %shard_map.115), channel_id=1, source_target_pairs={{0,32},{32,0},{64,96},{96,64},{128,160},{160,128},{192,224},{224,1... | collective-permute-start | bytes 786440 | tf_op jit(solution)/shard_map/ppermute | solution.py:224
  24.7 16.6 %collective-permute-start.11 = (bf16[1024,128]{1,0:T(8,128)(2,1)S(1)}, bf16[1024,128]{1,0:T(8,128)(2,1)S(1)}, u32[]{:S(2)}, u32[]{:S(2)}) collective-permute-start(bf16[1024,128]{1,0:T(8,128)(2,1)S(1)} %shard_map.116), channel_id=1, source_target_pairs={{0,1},{1,0},{2,3},{3,2},{4,5},{5,4},{6,7},{7,6},{8,9},{9,8},{10,11... | collective-permute-start | bytes 786440 | tf_op jit(solution)/shard_map/ppermute | solution.py:224
  24.8 10.5 %collective-permute-start.1 = (bf16[512,128]{1,0:T(8,128)(2,1)S(1)}, bf16[512,128]{1,0:T(8,128)(2,1)S(1)}, u32[]{:S(2)}, u32[]{:S(2)}) collective-permute-start(bf16[512,128]{1,0:T(8,128)(2,1)S(1)} %get-tuple-element.26.border), channel_id=1, source_target_pairs={{0,224},{32,64},{64,32},{96,128},{128,96},{160,192},{192,160},{224... | collective-permute-start | bytes 393224 | tf_op jit(solution)/shard_map/ppermute | solution.py:224
  26.0 9.4 %collective-permute-start.2 = (bf16[512,128]{1,0:T(8,128)(2,1)S(1)}, bf16[512,128]{1,0:T(8,128)(2,1)S(1)}, u32[]{:S(2)}, u32[]{:S(2)}) collective-permute-start(bf16[512,128]{1,0:T(8,128)(2,1)S(1)} %get-tuple-element.26.border), channel_id=1, source_target_pairs={{0,1},{1,0},{2,3},{3,2},{4,5},{5,4},{6,7},{7,6},{8,9},{9,8},{10,11... | collective-permute-start | bytes 393224 | tf_op jit(solution)/shard_map/ppermute | solution.py:224
  27.9 7.5 %collective-permute-start.3 = (bf16[512,128]{1,0:T(8,128)(2,1)S(1)}, bf16[512,128]{1,0:T(8,128)(2,1)S(1)}, u32[]{:S(2)}, u32[]{:S(2)}) collective-permute-start(bf16[512,128]{1,0:T(8,128)(2,1)S(1)} %get-tuple-element.26.border), channel_id=1, source_target_pairs={{0,7},{1,2},{2,1},{3,4},{4,3},{5,6},{6,5},{7,0},{8,15},{9,10},{10,... | collective-permute-start | bytes 393224 | tf_op jit(solution)/shard_map/ppermute | solution.py:224
  33.7 1.7 %copy-start.6 = (s32[32,128]{1,0:T(8,128)S(1)}, s32[32,128]{1,0:T(8,128)}, u32[]{:S(2)}) copy-start(s32[32,128]{1,0:T(8,128)} %param.13) | copy-start | bytes 49156
